TPU v7x, 256 devices: a whole 4x4x8 slice. The times are simulated.
256 devices in a mesh: gx: 4 (over z_hi), gy: 8 (over x, core), gz: 8 (over z_lo, y).
Axes of the slice: x: 4, y: 4, z: 8 (z_hi: 4, z_lo: 2; z = z_hi * 2 + z_lo), core: 2. Of those that a mesh axis runs over, the one named last changes fastest.
Arguments:
- state: float32 [7, 64, 128, 1024], P(None, 'gx', 'gy', 'gz'), may hold values from -1 to 4, as said below
- solver_owner: int32 [8, 8, 8], P('gy', 'gz'), may hold values from 0 to 15, as said below
- phi_prev: float32 [16, 8, 128, 1024], P('gx', None, 'gy', 'gz'), may hold values from -1.2 to 1.2
Outputs:
- new_state: float32 [7, 64, 128, 1024], P(None, 'gx', 'gy', 'gz')
- density_solver: float32 [16, 8, 128, 1024], P('gx', None, 'gy', 'gz')
- residual: float32 [64, 128, 1024], P('gx', 'gy', 'gz')
Inputs may be any that keep to these rules, and one draw needn't show every extreme that they name: `state`: field 0 lies in [1, 2], fields 1 to 3 in [-1, 1], field 4 in [2, 4], field 5 in [1, 2], field 6 in [0, 1]. `solver_owner`: entry b of line (j, k) is owner * 4 + slot, the owner being the gx index holding box b in the solver ownership. Codes within a line are distinct, so an owner holds at most 4 boxes of a line, and in every line some owner holds exactly 4.
All inputs are finite; a program needn't handle non-finite values.
Results may differ from a plain program's by a relative error of at most 0.00012.
Values sent between devices are 32-bit elements; how exact they have to be, the bound alone decides.
A program may use at most 64 MiB of HBM per device.

v0:
```python
import functools

import jax
import jax.numpy as jnp
from jax import lax
from jax.experimental import pallas as pl
from jax.experimental.pallas import tpu as pltpu
from jax.sharding import PartitionSpec as P

MESH = pl.DeviceIdType.MESH
GAMMA = 5.0 / 3.0
DTH = 0.04
FOURPIG = 2.0
NF = 7
CX, CY, CZ = 16, 16, 128
PITCH, BASE = 24, 8
ROWS = CX * PITCH + 8
HALF = 8
SLOTS = 4


def pressure(q5):
    return (GAMMA - 1.0) * jnp.maximum(q5, 0.1)


def speeds(get, dirs):
    inv = 1.0 / jnp.maximum(get(0), 0.25)
    sound = jnp.sqrt(GAMMA * pressure(get(5)) * inv)
    return [jnp.abs(get(d)) * inv + sound for d in dirs]


def interface_flux(get, speed_l, speed_r, d):
    def edge(k):
        a, b, c, e = get(k)
        v = 7.0 / 12.0 * (b + c) - 1.0 / 12.0 * (a + e)
        v = jnp.minimum(jnp.maximum(v, jnp.minimum(b, c)), jnp.maximum(b, c))
        return v, c - b

    half = 0.5 * jnp.maximum(speed_l, speed_r)
    e0, j0 = edge(0)
    ed, jd = edge(d)
    e5, j5 = edge(5)
    vel = ed / jnp.maximum(e0, 0.25)
    press = pressure(e5)
    out = [ed - half * j0]
    for k in (1, 2, 3):
        if k == d:
            out.append(ed * vel + press - half * jd)
        else:
            ek, jk = edge(k)
            out.append(ek * vel - half * jk)
    e4, j4 = edge(4)
    out.append((e4 + press) * vel - half * j4)
    out.append(e5 * vel - half * j5)
    e6, j6 = edge(6)
    out.append(e6 * vel - half * j6)
    return out


def lanes(shape=(CY, CZ)):
    return lax.broadcasted_iota(jnp.int32, shape, 1)


def rows_of(i):
    start = i * PITCH + BASE
    if not isinstance(i, int):
        start = pl.multiple_of(start, 8)
    return pl.ds(start, CY)


def z_shifted(q):
    return (pltpu.roll(q, 1, 1), q, pltpu.roll(q, CZ - 1, 1), pltpu.roll(q, CZ - 2, 1))


def each(n, body, unroll=1):
    def step(i, c):
        body(i)
        return c

    lax.fori_loop(0, n, step, 0, unroll=unroll)


def pack_z(load, count, dst):
    lane = lanes()

    def body(i, acc):
        here = (lane >= 8 * i) & (lane < 8 * i + 8)
        shift = lax.rem(8 * i + 4, CZ)
        return tuple(jnp.where(here, pltpu.roll(load(k, i), shift, 1), acc[k]) for k in range(count))

    acc = lax.fori_loop(0, CX, body, tuple(jnp.zeros((CY, CZ), jnp.float32) for _ in range(count)))
    for k in range(count):
        dst[k] = acc[k]


def kernel(n_gx, n_gy, n_gz, owner, state, phi_in, new_out, den_out, res_out,
           q1, q2, phi, sx, sy, sz, dd, fb, fym, tz, nst,
           xh, ysend, yrecv, zpack, zrecv,
           pb, pot, pin, pfirst, gl, gr, go, dsol,
           pxr, pys, pyr, pzs, pzr, res,
           m0, m1, m2, my, mz, mx,
           lsem, osem, hs, hr, ps, pr, ds_, dr, fs, fr, ms, mr):
    gx, gy, gz = lax.axis_index("gx"), lax.axis_index("gy"), lax.axis_index("gz")

    def at(axis, pos, n, off):
        return {axis: lax.rem(pos + (off + n), n)}

    x_lo, x_hi = at("gx", gx, n_gx, -1), at("gx", gx, n_gx, 1)
    y_lo, y_hi = at("gy", gy, n_gy, -1), at("gy", gy, n_gy, 1)
    z_lo, z_hi = at("gz", gz, n_gz, -1), at("gz", gz, n_gz, 1)

    def remote(src, dst, send, recv, dev):
        c = pltpu.make_async_remote_copy(src_ref=src, dst_ref=dst, send_sem=send, recv_sem=recv,
                                         device_id=dev, device_id_type=MESH)
        c.start()
        return c

    loads = {}
    for i in (0, 1, 14, 15, 2, 3, 4, 5, 6, 7, 8, 9, 10, 11, 12, 13):
        c = pltpu.make_async_copy(state.at[:, i], q1.at[:, rows_of(i)], lsem.at[i])
        c.start()
        loads[i] = c
    phi_load = pltpu.make_async_copy(phi_in, phi, lsem.at[CX])
    phi_load.start()

    barrier = pltpu.get_barrier_semaphore()
    peers = [at("gx", gx, n_gx, o) for o in range(1, n_gx)]
    peers += [at("gy", gy, n_gy, o) for o in range(1, n_gy)]
    peers += [at("gz", gz, n_gz, o) for o in range(1, n_gz)]
    for dev in peers:
        pl.semaphore_signal(barrier, inc=1, device_id=dev, device_id_type=MESH)
    pl.semaphore_wait(barrier, len(peers))

    pending = []

    def send_x(q, r):
        cs = []
        for j in (0, 1):
            cs.append(remote(q.at[:, rows_of(14 + j)], xh.at[r, 0, j], hs.at[r, j], hr.at[r, j], x_hi))
            cs.append(remote(q.at[:, rows_of(j)], xh.at[r, 1, j], hs.at[r, 2 + j], hr.at[r, 2 + j], x_lo))
        return cs

    def send_y(q, r):
        for k in range(NF):
            for j in (0, 1):
                ysend[r, 0, k, j] = q[k, pl.ds(BASE + j, CX, stride=PITCH), :]
                ysend[r, 1, k, j] = q[k, pl.ds(BASE + 14 + j, CX, stride=PITCH), :]
        return [remote(ysend.at[r, 1], yrecv.at[r, 0], hs.at[r, 4], hr.at[r, 4], y_hi),
                remote(ysend.at[r, 0], yrecv.at[r, 1], hs.at[r, 5], hr.at[r, 5], y_lo)]

    def send_z(q, r):
        pack_z(lambda k, i: q[k, rows_of(i), :], NF, zpack.at[r])
        return [remote(zpack.at[r], zrecv.at[r, 0], hs.at[r, 6], hr.at[r, 6], z_hi),
                remote(zpack.at[r], zrecv.at[r, 1], hs.at[r, 7], hr.at[r, 7], z_lo)]

    def interior(q):
        def speed_body(i):
            s = speeds(lambda k: q[k, rows_of(i), :], (1, 2, 3))
            sx[i] = s[0]
            sy[rows_of(i), :] = s[1]
            sz[i] = s[2]

        each(CX, speed_body)
        lane = lanes()
        inner = (lane >= 2) & (lane < CZ - 2)

        def z_body(i):
            s = sz[i]
            f = interface_flux(lambda k: z_shifted(q[k, rows_of(i), :]), s, pltpu.roll(s, CZ - 1, 1), 3)
            for k in range(NF):
                dd[k, i] = jnp.where(inner, pltpu.roll(f[k], 1, 1) - f[k], 0.0)

        each(CX, z_body)

        def x_flux(i):
            return interface_flux(lambda k: tuple(q[k, rows_of(i + o), :] for o in (-1, 0, 1, 2)), sx[i], sx[i + 1], 1)

        f = x_flux(1)
        for k in range(NF):
            fb[0, k] = f[k]

        def x_body(i, prev):
            f = x_flux(i)
            for k in range(NF):
                dd[k, i] = dd[k, i] + (prev[k] - f[k])
            return tuple(f)

        f = lax.fori_loop(2, 14, x_body, tuple(f))
        for k in range(NF):
            fb[1, k] = f[k]

    def yz_part(q, r, finish):
        lane = lanes()
        sub = lane & 7
        low = sub < 4

        def z_edge(get):
            s, = speeds(get, (3,))
            f = interface_flux(lambda k: z_shifted(get(k)), s, pltpu.roll(s, CZ - 1, 1), 3)
            return [pltpu.roll(f[k], 1, 1) - f[k] for k in range(NF)]

        left = z_edge(lambda k: jnp.where(low, zrecv[r, 0, k], zpack[r, k]))
        for k in range(NF):
            tz[k] = left[k]
        right = z_edge(lambda k: jnp.where(low, zpack[r, k], zrecv[r, 1, k]))
        for k in range(NF):
            tz[k] = jnp.where(low, right[k], tz[k])

        for k in range(NF):
            for j in (0, 1):
                q[k, pl.ds(BASE - 2 + j, CX, stride=PITCH), :] = yrecv[r, 0, k, j]
                q[k, pl.ds(BASE + CY + j, CX, stride=PITCH), :] = yrecv[r, 1, k, j]
        sy[pl.ds(BASE + CY, CX, stride=PITCH), :] = speeds(lambda k: yrecv[r, 1, k, 0], (2,))[0]
        s_l, = speeds(lambda k: yrecv[r, 0, k, 1], (2,))
        s_r, = speeds(lambda k: ysend[r, 0, k, 0], (2,))
        f = interface_flux(
            lambda k: (yrecv[r, 0, k, 0], yrecv[r, 0, k, 1], ysend[r, 0, k, 0], ysend[r, 0, k, 1]), s_l, s_r, 2)
        for k in range(NF):
            fym[k] = f[k]

        outer = (lane < 2) | (lane >= CZ - 2)
        first_row = lax.broadcasted_iota(jnp.int32, (CY, CZ), 0) == 0

        def y_body(i, done):
            at_ = i * PITCH + BASE
            f = interface_flux(lambda k: tuple(q[k, pl.ds(at_ + o, CY), :] for o in (-1, 0, 1, 2)),
                               sy[pl.ds(at_, CY), :], sy[pl.ds(at_ + 1, CY), :], 2)
            shift = lax.rem(CZ - 4 - 8 * i + CZ, CZ)
            t = []
            for k in range(NF):
                lower = jnp.where(first_row, fym[k, pl.ds(i, 1), :], pltpu.roll(f[k], 1, 0))
                edge = jnp.where(outer, pltpu.roll(tz[k], shift, 1), 0.0)
                t.append(dd[k, i] + ((lower - f[k]) + edge))
            if done:
                finish(i, t)
            else:
                for k in range(NF):
                    dd[k, i] = t[k]

        for i in (0, 14):
            def body(j, i=i):
                y_body(i + j, False)
            each(2, body)

        def body(j):
            y_body(2 + j, True)
        each(12, body)

    def x_part(q, r, finish):
        def get(i):
            if i < 0:
                return lambda k: xh[r, 0, i + 2, k]
            if i >= CX:
                return lambda k: xh[r, 1, i - CX, k]
            return lambda k: q[k, rows_of(i), :]

        def speed(i):
            return sx[i] if 0 <= i < CX else speeds(get(i), (1,))[0]

        def flux(i):
            g = [get(i + o) for o in (-1, 0, 1, 2)]
            return interface_flux(lambda k: tuple(h(k) for h in g), speed(i), speed(i + 1), 1)

        a = flux(-1)
        b = flux(0)
        finish(0, [dd[k, 0] + (a[k] - b[k]) for k in range(NF)])
        finish(1, [dd[k, 1] + (b[k] - fb[0, k]) for k in range(NF)])
        a = flux(14)
        finish(14, [dd[k, 14] + (fb[1, k] - a[k]) for k in range(NF)])
        b = flux(15)
        finish(15, [dd[k, 15] + (a[k] - b[k]) for k in range(NF)])

    def finish_first(i, t):
        for k in range(NF):
            q2[k, rows_of(i), :] = q1[k, rows_of(i), :] + DTH * t[k]

    def finish_new(i, t):
        for k in range(NF):
            nst[k, i] = 0.5 * q1[k, rows_of(i), :] + 0.5 * (q2[k, rows_of(i), :] + DTH * t[k])

    for i in (0, 1, 14, 15):
        loads[i].wait()
    xs = send_x(q1, 0)
    for i in range(2, 14):
        loads[i].wait()
    yzs = send_y(q1, 0) + send_z(q1, 0)
    pending += xs + yzs

    phi_load.wait()

    def is_code(box, slot):
        return jnp.where(owner[box] == gx * SLOTS + slot, 1.0, 0.0).astype(jnp.float32)

    masks = [[[is_code(lax.rem(gx + o, n_gx) * 2 + b, s) for s in range(SLOTS)] for b in (0, 1)] for o in range(4)]

    for o in (2, 1, 3, 0):
        def phi_body(j, o=o):
            rows = [phi[s, j] for s in range(SLOTS)]
            for b in (0, 1):
                m = masks[o][b]
                v = rows[0] * m[0]
                for s in range(1, SLOTS):
                    v = v + rows[s] * m[s]
                pb[o, b, j] = v
        each(HALF, phi_body)
    p1 = [remote(pb.at[2, 0], pfirst.at[0], ps.at[0], pr.at[0], x_hi),
          remote(pb.at[2, 1], pfirst.at[1], ps.at[1], pr.at[1], x_lo)]

    interior(q1)
    for c in yzs:
        c.wait_recv()
    yz_part(q1, 0, finish_first)
    for c in xs:
        c.wait_recv()
    x_part(q1, 0, finish_first)

    xs = send_x(q2, 1)
    yzs = send_y(q2, 1) + send_z(q2, 1)
    pending += xs + yzs

    p2 = [remote(pb.at[1, 1], pin.at[0, 1], ps.at[2], pr.at[2], x_hi),
          remote(pb.at[3, 0], pin.at[1, 0], ps.at[3], pr.at[3], x_lo)]
    for c in p1:
        c.wait_recv()

    def add_body(j):
        pb[1, 0, j] = pb[1, 0, j] + pfirst[0, j]
        pb[3, 1, j] = pb[3, 1, j] + pfirst[1, j]

    each(HALF, add_body)
    p2 += [remote(pb.at[1, 0], pin.at[0, 0], ps.at[4], pr.at[4], x_hi),
           remote(pb.at[3, 1], pin.at[1, 1], ps.at[5], pr.at[5], x_lo)]
    pending += p1 + p2

    interior(q2)
    for c in yzs:
        c.wait_recv()
    yz_part(q2, 1, finish_new)
    for c in xs:
        c.wait_recv()
    x_part(q2, 1, finish_new)

    def mass_body(i, acc):
        return acc + nst[0, i, 0:8, :] + nst[0, i, 8:16, :]

    m0[...] = lax.fori_loop(0, CX, mass_body, jnp.zeros((8, CZ), jnp.float32))

    d1 = [remote(nst.at[0, pl.ds(0, HALF)], gl.at[0], ds_.at[0], dr.at[0], x_hi),
          remote(nst.at[0, pl.ds(HALF, HALF)], gr.at[1], ds_.at[1], dr.at[1], x_lo),
          remote(nst.at[0, pl.ds(HALF, HALF)], gl.at[1], ds_.at[2], dr.at[2], x_hi),
          remote(nst.at[0, pl.ds(0, HALF)], gr.at[0], ds_.at[3], dr.at[3], x_lo)]
    out_state = pltpu.make_async_copy(nst, new_out, osem.at[0])
    out_state.start()

    def spread(src, dst, axis, pos, n, first):
        return [remote(src, dst.at[o - 1], ms.at[first + o - 1], mr.at[first + o - 1], at(axis, pos, n, o))
                for o in range(1, n)]

    m_y = spread(m0, my, "gy", gy, n_gy, 0)

    for c in p2:
        c.wait_recv()

    def pot_body(j):
        for b in (0, 1):
            pot[b * HALF + j] = pb[0, b, j] + (pin[0, b, j] + pin[1, b, j])

    each(HALF, pot_body)
    def row_body(i):
        pys[0, pl.ds(i, 1), :] = pot[i, 0:1, :]
        pys[1, pl.ds(i, 1), :] = pot[i, CY - 1:CY, :]

    each(CX, row_body)
    pack_z(lambda k, i: pot[i], 1, pzs)
    ph = [remote(pot.at[CX - 1], pxr.at[0], fs.at[0], fr.at[0], x_hi),
          remote(pot.at[0], pxr.at[1], fs.at[1], fr.at[1], x_lo),
          remote(pys.at[1], pyr.at[0], fs.at[2], fr.at[2], y_hi),
          remote(pys.at[0], pyr.at[1], fs.at[3], fr.at[3], y_lo),
          remote(pzs.at[0], pzr.at[0], fs.at[4], fr.at[4], z_hi),
          remote(pzs.at[0], pzr.at[1], fs.at[5], fr.at[5], z_lo)]
    pending += ph

    def gathered(copies, own, got, n, out):
        for c in copies:
            c.wait_recv()
        acc = own[...]
        for o in range(n - 1):
            acc = acc + got[o]
        out[...] = acc

    gathered(m_y, m0, my, n_gy, m1)
    m_z = spread(m1, mz, "gz", gz, n_gz, n_gy - 1)

    d1[0].wait_recv()
    d2 = [remote(gl.at[0], go.at[0], ds_.at[4], dr.at[4], x_hi)]
    d1[1].wait_recv()
    d2 += [remote(gr.at[1], go.at[1], ds_.at[5], dr.at[5], x_lo)]

    gathered(m_z, m1, mz, n_gz, m2)
    m_x = spread(m2, mx, "gx", gx, n_gx, n_gy + n_gz - 2)
    pending += m_y + m_z + m_x

    for c in ph:
        c.wait_recv()
    lane = lanes()
    row = lax.broadcasted_iota(jnp.int32, (CY, CZ), 0)
    halo = jnp.where((lane & 7) < 4, pzr[0, :, :], pzr[1, :, :])

    def lap(i, below, above):
        p = pot[i]
        h = pltpu.roll(halo, lax.rem(CZ - 4 - 8 * i + CZ, CZ), 1)
        z = pltpu.roll(jnp.where(lane == CZ - 1, h, p), 1, 1) + pltpu.roll(jnp.where(lane == 0, h, p), CZ - 1, 1)
        up = jnp.where(row == 0, pyr[0, pl.ds(i, 1), :], pltpu.roll(p, 1, 0))
        dn = jnp.where(row == CY - 1, pyr[1, pl.ds(i, 1), :], pltpu.roll(p, CY - 1, 0))
        res[i] = FOURPIG * nst[0, i] - (((below + above) + (up + dn) + z) - 6.0 * p)

    lap(0, pxr[0], pot[1])

    def lap_body(j):
        lap(j + 1, pot[j], pot[j + 2])
    each(CX - 2, lap_body)
    lap(CX - 1, pot[CX - 2], pxr[1])

    for c in m_x:
        c.wait_recv()
    total = m2[...]
    for o in range(n_gx - 1):
        total = total + mx[o]
    cells = float(CX * CY * CZ * n_gx * n_gy * n_gz)
    mean = jnp.sum(total) * (FOURPIG / cells)

    def mean_body(i):
        res[i] = res[i] - mean
    each(CX, mean_body)
    out_res = pltpu.make_async_copy(res, res_out, osem.at[1])
    out_res.start()

    for c in (d1[2], d1[3]):
        c.wait_recv()

    def is_box(o, b, s):
        return is_code(lax.rem(gx + o, n_gx) * 2 + b, s)

    near = [[(is_box(o, b, s)) for o in (0, 3, 1) for b in (0, 1)] for s in range(SLOTS)]

    def near_body(j):
        boxes = [nst[0, j], nst[0, HALF + j], gl[0, j], gl[1, j], gr[0, j], gr[1, j]]
        for s in range(SLOTS):
            v = boxes[0] * near[s][0]
            for t in range(1, 6):
                v = v + boxes[t] * near[s][t]
            dsol[s, j] = v
    each(HALF, near_body)
    far = [[is_box(2, b, s) for b in (0, 1)] for s in range(SLOTS)]
    for c in d2:
        c.wait_recv()

    def far_body(j):
        boxes = [go[0, j], go[1, j]]
        for s in range(SLOTS):
            dsol[s, j] = dsol[s, j] + (boxes[0] * far[s][0] + boxes[1] * far[s][1])
    each(HALF, far_body)
    out_den = pltpu.make_async_copy(dsol, den_out, osem.at[2])
    out_den.start()

    pending += d1 + d2
    for c in pending:
        c.wait_send()
    out_state.wait()
    out_res.wait()
    out_den.wait()


def solution(mesh):
    n_gx, n_gy, n_gz = mesh.shape["gx"], mesh.shape["gy"], mesh.shape["gz"]

    def on_device(state, solver_owner, phi_prev):
        f32 = jnp.float32
        V = lambda *s: pltpu.VMEM(s, f32)
        D = lambda *s: pltpu.SemaphoreType.DMA(s)
        n_mass = n_gx + n_gy + n_gz - 3
        anyspace = pl.BlockSpec(memory_space=pl.ANY)
        return pl.pallas_call(
            functools.partial(kernel, n_gx, n_gy, n_gz),
            out_shape=(
                jax.ShapeDtypeStruct(state.shape, f32),
                jax.ShapeDtypeStruct(phi_prev.shape, f32),
                jax.ShapeDtypeStruct(state.shape[1:], f32),
            ),
            in_specs=[pl.BlockSpec(memory_space=pltpu.SMEM), anyspace, anyspace],
            out_specs=(anyspace, anyspace, anyspace),
            scratch_shapes=[
                V(NF, ROWS, CZ), V(NF, ROWS, CZ), V(SLOTS, HALF, CY, CZ),
                V(CX, CY, CZ), V(ROWS, CZ), V(CX, CY, CZ), V(NF, CX, CY, CZ),
                V(2, NF, CY, CZ), V(NF, CX, CZ), V(NF, CY, CZ), V(NF, CX, CY, CZ),
                V(2, 2, 2, NF, CY, CZ), V(2, 2, NF, 2, CX, CZ), V(2, 2, NF, 2, CX, CZ),
                V(2, NF, CY, CZ), V(2, 2, NF, CY, CZ),
                V(4, 2, HALF, CY, CZ), V(CX, CY, CZ), V(2, 2, HALF, CY, CZ), V(2, HALF, CY, CZ),
                V(2, HALF, CY, CZ), V(2, HALF, CY, CZ), V(2, HALF, CY, CZ), V(SLOTS, HALF, CY, CZ),
                V(2, CY, CZ), V(2, CX, CZ), V(2, CX, CZ), V(1, CY, CZ), V(2, CY, CZ), V(CX, CY, CZ),
                V(8, CZ), V(8, CZ), V(8, CZ),
                V(n_gy - 1, 8, CZ), V(n_gz - 1, 8, CZ), V(n_gx - 1, 8, CZ),
                D(CX + 1), D(3), D(2, 8), D(2, 8), D(6), D(6), D(6), D(6), D(6), D(6), D(n_mass), D(n_mass),
            ],
            compiler_params=pltpu.CompilerParams(
                collective_id=0, has_side_effects=True, vmem_limit_bytes=32 * 1024 * 1024
            ),
            name="gas_step",
        )(solver_owner.reshape(-1), state, phi_prev)

    return jax.shard_map(
        on_device,
        mesh=mesh,
        in_specs=(P(None, "gx", "gy", "gz"), P("gy", "gz", None), P("gx", None, "gy", "gz")),
        out_specs=(P(None, "gx", "gy", "gz"), P("gx", None, "gy", "gz"), P("gx", "gy", "gz")),
        check_vma=False,
    )
```

profile of v0, /device:TPU:8, one launch (start us, length us, event | category | flops | bytes accessed | tf_op | source)
XLA Modules:
  0.0 57.8 jit_solution(2313710828386689887)
XLA Ops:
  0.6 0.0 copy-start.2
  0.6 0.6 %copy-done.2 = s32[1,1,8]{2,1,0:T(1,128)S(1)} copy-done((s32[1,1,8]{2,1,0:T(1,128)S(1)}, s32[1,1,8]{2,1,0:T(1,128)}, u32[]{:S(2)}) %copy-start.2) | copy-done | bytes 56
  1.3 0.0 copy-start
  1.3 1.2 %copy-done = f32[7,16,16,128]{3,2,1,0:T(8,128)S(1)} copy-done((f32[7,16,16,128]{3,2,1,0:T(8,128)S(1)}, f32[7,16,16,128]{3,2,1,0:T(8,128)}, u32[]{:S(2)}) %copy-start) | copy-done | bytes 917528
  2.5 0.0 copy-start.1
  2.5 0.9 %copy-done.1 = f32[4,8,16,128]{3,2,1,0:T(8,128)S(1)} copy-done((f32[4,8,16,128]{3,2,1,0:T(8,128)S(1)}, f32[4,8,16,128]{3,2,1,0:T(8,128)}, u32[]{:S(2)}) %copy-start.1) | copy-done | bytes 262168
  3.4 52.1 %gas_step.1 = (f32[7,16,16,128]{3,2,1,0:T(8,128)S(1)}, f32[4,8,16,128]{3,2,1,0:T(8,128)S(1)}, f32[16,16,128]{2,1,0:T(8,128)S(1)}) custom-call(s32[8]{0:T(128)S(1)} %bitcast.1, f32[7,16,16,128]{3,2,1,0:T(8,128)S(1)} %copy-done, f32[4,8,16,128]{3,2,1,0:T(8,128)S(1)} %copy-done.1), custom_call_target="tpu_custom_call" | custom-call | tf_op jit(solution)/shard_map/gas_step/pallas_call | solution.py:483
  55.5 0.9 %copy.9 = f32[7,16,16,128]{3,2,1,0:T(8,128)} copy(f32[7,16,16,128]{3,2,1,0:T(8,128)S(1)} %get-tuple-element.6) | data formatting | bytes 1835008
  56.5 0.7 %copy.10 = f32[4,8,16,128]{3,2,1,0:T(8,128)} copy(f32[4,8,16,128]{3,2,1,0:T(8,128)S(1)} %get-tuple-element.7) | data formatting | bytes 524288
  57.2 0.7 %copy.11 = f32[16,16,128]{2,1,0:T(8,128)} copy(f32[16,16,128]{2,1,0:T(8,128)S(1)} %get-tuple-element.8) | data formatting | bytes 262144
Async XLA Ops:
  0.6 0.7 %copy-start.2 = (s32[1,1,8]{2,1,0:T(1,128)S(1)}, s32[1,1,8]{2,1,0:T(1,128)}, u32[]{:S(2)}) copy-start(s32[1,1,8]{2,1,0:T(1,128)} %param.4) | copy-start | bytes 100
  1.3 1.2 %copy-start = (f32[7,16,16,128]{3,2,1,0:T(8,128)S(1)}, f32[7,16,16,128]{3,2,1,0:T(8,128)}, u32[]{:S(2)}) copy-start(f32[7,16,16,128]{3,2,1,0:T(8,128)} %state.1) | copy-start | bytes 2752516
  2.5 0.9 %copy-start.1 = (f32[4,8,16,128]{3,2,1,0:T(8,128)S(1)}, f32[4,8,16,128]{3,2,1,0:T(8,128)}, u32[]{:S(2)}) copy-start(f32[4,8,16,128]{3,2,1,0:T(8,128)} %phi_in.1) | copy-start | bytes 786436
where the time goes:
time: 58 us; the launch traced here: 57.8 us
  Pallas kernels  52.1 us (90%)
  local copies, waits for them, and re-layouts  5.06 us (9%)
  between operations  0.65 us (1%)
    pallas_call x1, Pallas kernels, on_device(): pl.pallas_call(functools.partial(kernel, n_gx, n_gy, n_gz), out_shape=(ja...  52.1 us
    unnamed x9, local copies, waits for them, and re-layouts  5.06 us

commit v1 on v0

v1 whole, which is shorter than its diff:
```python
import functools

import jax
import jax.numpy as jnp
from jax import lax
from jax.experimental import pallas as pl
from jax.experimental.pallas import tpu as pltpu
from jax.sharding import PartitionSpec as P

MESH = pl.DeviceIdType.MESH
GAMMA = 5.0 / 3.0
DTH = 0.04
FOURPIG = 2.0
NF = 7
CX, CY, CZ = 16, 16, 128
PITCH, BASE = 24, 8
ROWS = CX * PITCH + 8
HALF = 8
SLOTS = 4
UN = 2


def pressure(q5):
    return (GAMMA - 1.0) * jnp.maximum(q5, 0.1)


def speeds(get, dirs):
    inv = 1.0 / jnp.maximum(get(0), 0.25)
    sound = jnp.sqrt(GAMMA * pressure(get(5)) * inv)
    return [jnp.abs(get(d)) * inv + sound for d in dirs]


def interface_flux(get, speed_l, speed_r, d):
    def edge(k):
        a, b, c, e = get(k)
        v = 7.0 / 12.0 * (b + c) - 1.0 / 12.0 * (a + e)
        v = jnp.minimum(jnp.maximum(v, jnp.minimum(b, c)), jnp.maximum(b, c))
        return v, c - b

    half = 0.5 * jnp.maximum(speed_l, speed_r)
    e0, j0 = edge(0)
    ed, jd = edge(d)
    e5, j5 = edge(5)
    vel = ed / jnp.maximum(e0, 0.25)
    press = pressure(e5)
    out = [ed - half * j0]
    for k in (1, 2, 3):
        if k == d:
            out.append(ed * vel + press - half * jd)
        else:
            ek, jk = edge(k)
            out.append(ek * vel - half * jk)
    e4, j4 = edge(4)
    out.append((e4 + press) * vel - half * j4)
    out.append(e5 * vel - half * j5)
    e6, j6 = edge(6)
    out.append(e6 * vel - half * j6)
    return out


def lanes(shape=(CY, CZ)):
    return lax.broadcasted_iota(jnp.int32, shape, 1)


def rows_of(i):
    start = i * PITCH + BASE
    if not isinstance(i, int):
        start = pl.multiple_of(start, 8)
    return pl.ds(start, CY)


def z_shifted(q):
    return (pltpu.roll(q, 1, 1), q, pltpu.roll(q, CZ - 1, 1), pltpu.roll(q, CZ - 2, 1))


def each(n, body, unroll=1):
    def step(i, c):
        body(i)
        return c

    lax.fori_loop(0, n, step, 0, unroll=unroll)


def pack_z(load, acc, slabs, unroll):
    lane = lanes()

    def put(i, acc, shift):
        here = (lane >= 8 * i) & (lane < 8 * i + 8)
        return tuple(jnp.where(here, pltpu.roll(load(k, i), shift, 1), a) for k, a in enumerate(acc))

    if isinstance(slabs, tuple):
        for i in slabs:
            acc = put(i, acc, (8 * i + 4) % CZ)
        return acc
    return lax.fori_loop(slabs.start, slabs.stop, lambda i, a: put(i, a, lax.rem(8 * i + 4, CZ)), acc, unroll=unroll)


def blank(count):
    return tuple(jnp.zeros((CY, CZ), jnp.float32) for _ in range(count))


def move_out(*refs):
    n = (len(refs) - 1) // 2
    sem = refs[-1]
    copies = [pltpu.make_async_copy(refs[i], refs[n + i], sem.at[i]) for i in range(n)]
    for c in copies:
        c.start()
    for c in copies:
        c.wait()


def kernel(n_gx, n_gy, n_gz, owner_in, state, phi_in, nst, dsol, res,
           owner_ref, q1, q2, phi, sx, sy, sz, dd, fb, fym, tz,
           xh, ysend, yrecv, zpack, zsend, zrecv,
           pb, pot, pin, pfirst, gl, gr, go,
           pxr, pys, pyr, pzs, pzr,
           m0, m1, m2, mx, my, mz,
           lsem, hs, hr, ps, pr, ds_, dr, fs, fr, ms, mr):
    gx, gy, gz = lax.axis_index("gx"), lax.axis_index("gy"), lax.axis_index("gz")

    def at(axis, pos, n, off):
        return {axis: lax.rem(pos + (off + n), n)}

    x_lo, x_hi = at("gx", gx, n_gx, -1), at("gx", gx, n_gx, 1)
    y_lo, y_hi = at("gy", gy, n_gy, -1), at("gy", gy, n_gy, 1)
    z_lo, z_hi = at("gz", gz, n_gz, -1), at("gz", gz, n_gz, 1)

    def remote(src, dst, send, recv, dev):
        c = pltpu.make_async_remote_copy(src_ref=src, dst_ref=dst, send_sem=send, recv_sem=recv,
                                         device_id=dev, device_id_type=MESH)
        c.start()
        return c

    loads = {}
    for i in (0, 1, 14, 15, 2, 3, 4, 5, 6, 7, 8, 9, 10, 11, 12, 13):
        c = pltpu.make_async_copy(state.at[:, i], q1.at[:, rows_of(i)], lsem.at[i])
        c.start()
        loads[i] = c
    phi_load = pltpu.make_async_copy(phi_in, phi, lsem.at[CX])
    phi_load.start()
    owner_load = pltpu.make_async_copy(owner_in, owner_ref, lsem.at[CX + 1])
    owner_load.start()

    barrier = pltpu.get_barrier_semaphore()
    peers = [x_lo, x_hi, y_lo, y_hi, z_lo, z_hi, at("gy", gy, n_gy, n_gy // 2), at("gz", gz, n_gz, n_gz // 2)]
    for dev in peers:
        pl.semaphore_signal(barrier, inc=1, device_id=dev, device_id_type=MESH)

    pending = []

    def send_x(q, r):
        cs = []
        for j in (0, 1):
            cs.append(remote(q.at[:, rows_of(14 + j)], xh.at[r, 0, j], hs.at[r, j], hr.at[r, j], x_hi))
            cs.append(remote(q.at[:, rows_of(j)], xh.at[r, 1, j], hs.at[r, 2 + j], hr.at[r, 2 + j], x_lo))
        return cs

    def pack_y(q, r):
        for k in range(NF):
            for j in (0, 1):
                ysend[r, 0, k, j] = q[k, pl.ds(BASE + j, CX, stride=PITCH), :]
                ysend[r, 1, k, j] = q[k, pl.ds(BASE + 14 + j, CX, stride=PITCH), :]

    def pack_inner(q, r):
        acc = pack_z(lambda k, i: q[k, rows_of(i), :], blank(NF), range(2, CX - 2), 6)
        for k in range(NF):
            zpack[r, k] = acc[k]

    def pack_outer(q, r):
        acc = pack_z(lambda k, i: q[k, rows_of(i), :], tuple(zpack[r, k] for k in range(NF)), (0, 1, 14, 15), 1)
        low = (lanes((8, CZ)) & 7) < 4
        for k in range(NF):
            zpack[r, k] = acc[k]
            top, bottom = acc[k][0:8], acc[k][8:16]
            zsend[r, 1, k] = jnp.where(low, top, pltpu.roll(bottom, 4, 1))
            zsend[r, 0, k] = jnp.where(low, pltpu.roll(top, CZ - 4, 1), bottom)

    def send_y(r):
        return [remote(ysend.at[r, 1], yrecv.at[r, 0], hs.at[r, 4], hr.at[r, 4], y_hi),
                remote(ysend.at[r, 0], yrecv.at[r, 1], hs.at[r, 5], hr.at[r, 5], y_lo)]

    def send_z(r):
        return [remote(zsend.at[r, 1], zrecv.at[r, 0], hs.at[r, 6], hr.at[r, 6], z_hi),
                remote(zsend.at[r, 0], zrecv.at[r, 1], hs.at[r, 7], hr.at[r, 7], z_lo)]

    def interior(q):
        def speed_body(i):
            s = speeds(lambda k: q[k, rows_of(i), :], (1, 2, 3))
            sx[i] = s[0]
            sy[rows_of(i), :] = s[1]
            sz[i] = s[2]

        each(CX, speed_body, UN)
        lane = lanes()
        inner = (lane >= 2) & (lane < CZ - 2)

        def z_body(i):
            s = sz[i]
            f = interface_flux(lambda k: z_shifted(q[k, rows_of(i), :]), s, pltpu.roll(s, CZ - 1, 1), 3)
            for k in range(NF):
                dd[k, i] = jnp.where(inner, pltpu.roll(f[k], 1, 1) - f[k], 0.0)

        each(CX, z_body, UN)

        def x_flux(i):
            return interface_flux(lambda k: tuple(q[k, rows_of(i + o), :] for o in (-1, 0, 1, 2)), sx[i], sx[i + 1], 1)

        f = x_flux(1)
        for k in range(NF):
            fb[0, k] = f[k]

        def x_body(i, prev):
            f = x_flux(i)
            for k in range(NF):
                dd[k, i] = dd[k, i] + (prev[k] - f[k])
            return tuple(f)

        f = lax.fori_loop(2, 14, x_body, tuple(f), unroll=UN)
        for k in range(NF):
            fb[1, k] = f[k]

    def y_part(q, r):
        for k in range(NF):
            for j in (0, 1):
                q[k, pl.ds(BASE - 2 + j, CX, stride=PITCH), :] = yrecv[r, 0, k, j]
                q[k, pl.ds(BASE + CY + j, CX, stride=PITCH), :] = yrecv[r, 1, k, j]
        sy[pl.ds(BASE + CY, CX, stride=PITCH), :] = speeds(lambda k: yrecv[r, 1, k, 0], (2,))[0]
        s_l, = speeds(lambda k: yrecv[r, 0, k, 1], (2,))
        s_r, = speeds(lambda k: ysend[r, 0, k, 0], (2,))
        f = interface_flux(
            lambda k: (yrecv[r, 0, k, 0], yrecv[r, 0, k, 1], ysend[r, 0, k, 0], ysend[r, 0, k, 1]), s_l, s_r, 2)
        for k in range(NF):
            fym[k] = f[k]
        first_row = lax.broadcasted_iota(jnp.int32, (CY, CZ), 0) == 0

        def y_body(i):
            at_ = i * PITCH + BASE
            f = interface_flux(lambda k: tuple(q[k, pl.ds(at_ + o, CY), :] for o in (-1, 0, 1, 2)),
                               sy[pl.ds(at_, CY), :], sy[pl.ds(at_ + 1, CY), :], 2)
            for k in range(NF):
                lower = jnp.where(first_row, fym[k, pl.ds(i, 1), :], pltpu.roll(f[k], 1, 0))
                dd[k, i] = dd[k, i] + (lower - f[k])

        each(CX, y_body, UN)

    def z_part(r):
        low = (lanes() & 7) < 4

        def z_edge(cells):
            s, = speeds(lambda k: cells[k], (3,))
            f = interface_flux(lambda k: z_shifted(cells[k]), s, pltpu.roll(s, CZ - 1, 1), 3)
            return [pltpu.roll(f[k], 1, 1) - f[k] for k in range(NF)]

        def from_left(k):
            m = zrecv[r, 0, k]
            return jnp.concatenate([m, pltpu.roll(m, CZ - 4, 1)], axis=0)

        def from_right(k):
            m = zrecv[r, 1, k]
            return jnp.concatenate([pltpu.roll(m, 4, 1), m], axis=0)

        left = z_edge([jnp.where(low, from_left(k), zpack[r, k]) for k in range(NF)])
        for k in range(NF):
            tz[k] = left[k]
        right = z_edge([jnp.where(low, zpack[r, k], from_right(k)) for k in range(NF)])
        for k in range(NF):
            tz[k] = jnp.where(low, right[k], tz[k])

    def tendency(i, k):
        lane = lanes()
        outer = (lane < 2) | (lane >= CZ - 2)
        shift = (2 * CZ - 4 - 8 * i) % CZ if isinstance(i, int) else lax.rem(2 * CZ - 4 - 8 * i, CZ)
        return dd[k, i] + jnp.where(outer, pltpu.roll(tz[k], shift, 1), 0.0)

    def x_part(q, r, finish):
        def get(i):
            if i < 0:
                return lambda k: xh[r, 0, i + 2, k]
            if i >= CX:
                return lambda k: xh[r, 1, i - CX, k]
            return lambda k: q[k, rows_of(i), :]

        def speed(i):
            return sx[i] if 0 <= i < CX else speeds(get(i), (1,))[0]

        def flux(i):
            g = [get(i + o) for o in (-1, 0, 1, 2)]
            return interface_flux(lambda k: tuple(h(k) for h in g), speed(i), speed(i + 1), 1)

        a = flux(-1)
        b = flux(0)
        finish(0, [tendency(0, k) + (a[k] - b[k]) for k in range(NF)])
        finish(1, [tendency(1, k) + (b[k] - fb[0, k]) for k in range(NF)])
        a = flux(14)
        finish(14, [tendency(14, k) + (fb[1, k] - a[k]) for k in range(NF)])
        b = flux(15)
        finish(15, [tendency(15, k) + (a[k] - b[k]) for k in range(NF)])

    def rest(finish):
        def body(j):
            finish(2 + j, [tendency(2 + j, k) for k in range(NF)])
        each(CX - 4, body, UN)

    def finish_first(i, t):
        for k in range(NF):
            q2[k, rows_of(i), :] = q1[k, rows_of(i), :] + DTH * t[k]

    def finish_new(i, t):
        for k in range(NF):
            nst[k, i] = 0.5 * q1[k, rows_of(i), :] + 0.5 * (q2[k, rows_of(i), :] + DTH * t[k])

    for i in range(CX):
        loads[i].wait()
    pack_inner(q1, 0)
    pack_outer(q1, 0)
    pl.semaphore_wait(barrier, len(peers))
    zs = send_z(0)
    xs = send_x(q1, 0)
    pack_y(q1, 0)
    ys = send_y(0)
    pending += xs + ys + zs

    phi_load.wait()
    owner_load.wait()

    def is_code(box, slot):
        return jnp.where(owner_ref[0, 0, box] == gx * SLOTS + slot, 1.0, 0.0).astype(jnp.float32)

    masks = [[[is_code(lax.rem(gx + o, n_gx) * 2 + b, s) for s in range(SLOTS)] for b in (0, 1)] for o in range(4)]

    for o in (2, 1, 3, 0):
        def phi_body(j, o=o):
            rows = [phi[s, j] for s in range(SLOTS)]
            for b in (0, 1):
                m = masks[o][b]
                v = rows[0] * m[0]
                for s in range(1, SLOTS):
                    v = v + rows[s] * m[s]
                pb[o, b, j] = v
        each(HALF, phi_body)
    interior(q1)
    for c in ys:
        c.wait_recv()
    y_part(q1, 0)
    p1 = [remote(pb.at[2, 0], pfirst.at[0], ps.at[0], pr.at[0], x_hi),
          remote(pb.at[2, 1], pfirst.at[1], ps.at[1], pr.at[1], x_lo)]
    for c in zs:
        c.wait_recv()
    z_part(0)
    rest(finish_first)
    pack_inner(q2, 1)
    for c in xs:
        c.wait_recv()
    x_part(q1, 0, finish_first)

    pack_outer(q2, 1)
    zs = send_z(1)
    xs = send_x(q2, 1)
    pack_y(q2, 1)
    ys = send_y(1)
    pending += xs + ys + zs

    interior(q2)
    for c in ys:
        c.wait_recv()
    y_part(q2, 1)
    p2 = [remote(pb.at[1, 1], pin.at[0, 1], ps.at[2], pr.at[2], x_hi),
          remote(pb.at[3, 0], pin.at[1, 0], ps.at[3], pr.at[3], x_lo)]
    for c in p1:
        c.wait_recv()

    def add_body(j):
        pb[1, 0, j] = pb[1, 0, j] + pfirst[0, j]
        pb[3, 1, j] = pb[3, 1, j] + pfirst[1, j]

    each(HALF, add_body)
    p2 += [remote(pb.at[1, 0], pin.at[0, 0], ps.at[4], pr.at[4], x_hi),
           remote(pb.at[3, 1], pin.at[1, 1], ps.at[5], pr.at[5], x_lo)]
    pending += p1 + p2
    for c in zs:
        c.wait_recv()
    z_part(1)
    rest(finish_new)
    for c in xs:
        c.wait_recv()
    x_part(q2, 1, finish_new)

    d1 = [remote(nst.at[0, pl.ds(0, HALF)], gl.at[0], ds_.at[0], dr.at[0], x_hi),
          remote(nst.at[0, pl.ds(HALF, HALF)], gr.at[1], ds_.at[1], dr.at[1], x_lo),
          remote(nst.at[0, pl.ds(HALF, HALF)], gl.at[1], ds_.at[2], dr.at[2], x_hi),
          remote(nst.at[0, pl.ds(0, HALF)], gr.at[0], ds_.at[3], dr.at[3], x_lo)]

    def mass_body(i, acc):
        return acc + nst[0, i, 0:8, :] + nst[0, i, 8:16, :]

    m0[...] = lax.fori_loop(0, CX, mass_body, jnp.zeros((8, CZ), jnp.float32), unroll=4)

    def spread(src, dst, devices, first):
        return [remote(src, dst.at[t], ms.at[first + t], mr.at[first + t], dev) for t, dev in enumerate(devices)]

    def gathered(copies, own, got, n):
        for c in copies:
            c.wait_recv()
        acc = own[...]
        for o in range(n - 1):
            acc = acc + got[o]
        return acc

    n_zy = n_gz // 2
    along_y = [{"gz": (gz // n_zy) * n_zy + lax.rem(gz + o, n_zy)} for o in range(1, n_zy)]
    along_z = [{**at("gx", gx, n_gx, o), **at("gz", gz, n_gz, h * n_zy)}
               for o in range(n_gx) for h in (0, 1) if o + h > 0]
    m_x = spread(m0, mx, [at("gy", gy, n_gy, o) for o in range(1, n_gy)], 0)

    m1[...] = gathered(m_x, m0, mx, n_gy)
    m_y = spread(m1, my, along_y, n_gy - 1)
    m2[...] = gathered(m_y, m1, my, n_zy)
    m_z = spread(m2, mz, along_z, n_gy + n_zy - 2)
    pending += m_y + m_z + m_x

    for c in p2:
        c.wait_recv()

    def pot_body(j):
        for b in (0, 1):
            pot[b * HALF + j] = pb[0, b, j] + (pin[0, b, j] + pin[1, b, j])

    each(HALF, pot_body)
    def row_body(i):
        pys[0, pl.ds(i, 1), :] = pot[i, 0:1, :]
        pys[1, pl.ds(i, 1), :] = pot[i, CY - 1:CY, :]

    each(CX, row_body)
    pzs[0] = pack_z(lambda k, i: pot[i], blank(1), range(0, CX), 4)[0]
    ph = [remote(pot.at[CX - 1], pxr.at[0], fs.at[0], fr.at[0], x_hi),
          remote(pot.at[0], pxr.at[1], fs.at[1], fr.at[1], x_lo),
          remote(pys.at[1], pyr.at[0], fs.at[2], fr.at[2], y_hi),
          remote(pys.at[0], pyr.at[1], fs.at[3], fr.at[3], y_lo),
          remote(pzs.at[0], pzr.at[0], fs.at[4], fr.at[4], z_hi),
          remote(pzs.at[0], pzr.at[1], fs.at[5], fr.at[5], z_lo)]
    pending += ph

    d1[0].wait_recv()
    d2 = [remote(gl.at[0], go.at[0], ds_.at[4], dr.at[4], x_hi)]
    d1[1].wait_recv()
    d2 += [remote(gr.at[1], go.at[1], ds_.at[5], dr.at[5], x_lo)]

    for c in ph:
        c.wait_recv()
    lane = lanes()
    row = lax.broadcasted_iota(jnp.int32, (CY, CZ), 0)
    halo = jnp.where((lane & 7) < 4, pzr[0, :, :], pzr[1, :, :])

    def lap(i, below, above):
        p = pot[i]
        h = pltpu.roll(halo, lax.rem(CZ - 4 - 8 * i + CZ, CZ), 1)
        z = pltpu.roll(jnp.where(lane == CZ - 1, h, p), 1, 1) + pltpu.roll(jnp.where(lane == 0, h, p), CZ - 1, 1)
        up = jnp.where(row == 0, pyr[0, pl.ds(i, 1), :], pltpu.roll(p, 1, 0))
        dn = jnp.where(row == CY - 1, pyr[1, pl.ds(i, 1), :], pltpu.roll(p, CY - 1, 0))
        res[i] = FOURPIG * nst[0, i] - (((below + above) + (up + dn) + z) - 6.0 * p)

    lap(0, pxr[0], pot[1])

    def lap_body(j):
        lap(j + 1, pot[j], pot[j + 2])
    each(CX - 2, lap_body, 7)
    lap(CX - 1, pot[CX - 2], pxr[1])

    total = gathered(m_z, m2, mz, len(along_z) + 1)
    cells = float(CX * CY * CZ * n_gx * n_gy * n_gz)
    mean = jnp.sum(total) * (FOURPIG / cells)

    def mean_body(i):
        res[i] = res[i] - mean
    each(CX, mean_body)

    for c in (d1[2], d1[3]):
        c.wait_recv()

    def is_box(o, b, s):
        return is_code(lax.rem(gx + o, n_gx) * 2 + b, s)

    near = [[(is_box(o, b, s)) for o in (0, 3, 1) for b in (0, 1)] for s in range(SLOTS)]

    def near_body(j):
        boxes = [nst[0, j], nst[0, HALF + j], gl[0, j], gl[1, j], gr[0, j], gr[1, j]]
        for s in range(SLOTS):
            v = boxes[0] * near[s][0]
            for t in range(1, 6):
                v = v + boxes[t] * near[s][t]
            dsol[s, j] = v
    each(HALF, near_body)
    far = [[is_box(2, b, s) for b in (0, 1)] for s in range(SLOTS)]
    for c in d2:
        c.wait_recv()

    def far_body(j):
        boxes = [go[0, j], go[1, j]]
        for s in range(SLOTS):
            dsol[s, j] = dsol[s, j] + (boxes[0] * far[s][0] + boxes[1] * far[s][1])
    each(HALF, far_body)

    pending += d1 + d2
    for c in pending:
        c.wait_send()


def solution(mesh):
    n_gx, n_gy, n_gz = mesh.shape["gx"], mesh.shape["gy"], mesh.shape["gz"]

    def on_device(state, solver_owner, phi_prev):
        f32 = jnp.float32
        V = lambda *s: pltpu.VMEM(s, f32)
        D = lambda *s: pltpu.SemaphoreType.DMA(s)
        n_mass = 2 * n_gx + n_gy + n_gz // 2 - 3
        hbm = pl.BlockSpec(memory_space=pltpu.HBM)
        vmem = pl.BlockSpec(memory_space=pltpu.VMEM)
        outs = pl.pallas_call(
            functools.partial(kernel, n_gx, n_gy, n_gz),
            out_shape=(
                jax.ShapeDtypeStruct(state.shape, f32),
                jax.ShapeDtypeStruct(phi_prev.shape, f32),
                jax.ShapeDtypeStruct(state.shape[1:], f32),
            ),
            in_specs=[hbm, hbm, hbm],
            out_specs=(vmem, vmem, vmem),
            scratch_shapes=[
                pltpu.SMEM((1, 1, 8), jnp.int32),
                V(NF, ROWS, CZ), V(NF, ROWS, CZ), V(SLOTS, HALF, CY, CZ),
                V(CX, CY, CZ), V(ROWS, CZ), V(CX, CY, CZ), V(NF, CX, CY, CZ),
                V(2, NF, CY, CZ), V(NF, CX, CZ), V(NF, CY, CZ),
                V(2, 2, 2, NF, CY, CZ), V(2, 2, NF, 2, CX, CZ), V(2, 2, NF, 2, CX, CZ),
                V(2, NF, CY, CZ), V(2, 2, NF, 8, CZ), V(2, 2, NF, 8, CZ),
                V(4, 2, HALF, CY, CZ), V(CX, CY, CZ), V(2, 2, HALF, CY, CZ), V(2, HALF, CY, CZ),
                V(2, HALF, CY, CZ), V(2, HALF, CY, CZ), V(2, HALF, CY, CZ),
                V(2, CY, CZ), V(2, CX, CZ), V(2, CX, CZ), V(1, CY, CZ), V(2, CY, CZ),
                V(8, CZ), V(8, CZ), V(8, CZ),
                V(n_gy - 1, 8, CZ), V(n_gz // 2 - 1, 8, CZ), V(2 * n_gx - 1, 8, CZ),
                D(CX + 2), D(2, 8), D(2, 8), D(6), D(6), D(6), D(6), D(6), D(6), D(n_mass), D(n_mass),
            ],
            compiler_params=pltpu.CompilerParams(
                collective_id=0, has_side_effects=True, vmem_limit_bytes=32 * 1024 * 1024
            ),
            name="gas_step",
        )(
            pltpu.with_memory_space_constraint(solver_owner, pltpu.HBM),
            pltpu.with_memory_space_constraint(state, pltpu.HBM),
            pltpu.with_memory_space_constraint(phi_prev, pltpu.HBM),
        )
        return pl.pallas_call(
            move_out,
            out_shape=tuple(jax.ShapeDtypeStruct(o.shape, f32) for o in outs),
            in_specs=[vmem] * 3,
            out_specs=(hbm,) * 3,
            scratch_shapes=[D(3)],
            compiler_params=pltpu.CompilerParams(has_side_effects=True, vmem_limit_bytes=4 * 1024 * 1024),
            name="move_out",
        )(*outs)

    return jax.shard_map(
        on_device,
        mesh=mesh,
        in_specs=(P(None, "gx", "gy", "gz"), P("gy", "gz", None), P("gx", None, "gy", "gz")),
        out_specs=(P(None, "gx", "gy", "gz"), P("gx", None, "gy", "gz"), P("gx", "gy", "gz")),
        check_vma=False,
    )
```

time: 58 us -> 44.6 us (0.77)
  the two profiles are of different devices: /device:TPU:8 before, /device:TPU:1 now
where the time goes in v1:
time: 44.6 us; the launch traced here: 44.4 us
  Pallas kernels  43.8 us (98%)
  between operations  0.64 us (1%)
    pallas_call x1, Pallas kernels, on_device(): pl.pallas_call(functools.partial(kernel, n_gx, n_gy, n_gz), out_shape=(ja...  42.7 us
    pallas_call x1, Pallas kernels, on_device(): pl.pallas_call(move_out, out_shape=tuple((jax.ShapeDtypeStruct(o.shape, f...  1.07 us

profile of v1, /device:TPU:1, one launch (start us, length us, event | category | flops | bytes accessed | tf_op | source)
XLA Modules:
  0.0 44.4 jit_solution(10345467043950585479)
XLA Ops:
  0.6 42.7 %gas_step.1 = (f32[7,16,16,128]{3,2,1,0:T(8,128)S(1)}, f32[4,8,16,128]{3,2,1,0:T(8,128)S(1)}, f32[16,16,128]{2,1,0:T(8,128)S(1)}) custom-call(s32[1,1,8]{2,1,0:T(1,128)} %owner_in.1, f32[7,16,16,128]{3,2,1,0:T(8,128)} %state.1, f32[4,8,16,128]{3,2,1,0:T(8,128)} %phi_in.1), custom_call_target="tpu_custom_call" | custom-call | tf_op jit(solution)/shard_map/gas_step/pallas_call | solution.py:518
  43.3 1.1 %move_out.1 = (f32[7,16,16,128]{3,2,1,0:T(8,128)}, f32[4,8,16,128]{3,2,1,0:T(8,128)}, f32[16,16,128]{2,1,0:T(8,128)}) custom-call(f32[7,16,16,128]{3,2,1,0:T(8,128)S(1)} %get-tuple-element.6.refs_0_, f32[4,8,16,128]{3,2,1,0:T(8,128)S(1)} %get-tuple-element.7.refs_1_, f32[16,16,128]{2,1,0:T(8,128)S(1)} %get-tuple-element.8.refs_2_), custom_call_target="tpu_custom_call" | custom-call | tf_op jit(solution)/shard_map/move_out/pallas_call | solution.py:550

commit v2 on v1

--- a/solution.py
+++ b/solution.py
@@ -102,11 +102,11 @@
 def move_out(*refs):
     n = (len(refs) - 1) // 2
     sem = refs[-1]
-    copies = [pltpu.make_async_copy(refs[i], refs[n + i], sem.at[i]) for i in range(n)]
-    for c in copies:
-        c.start()
-    for c in copies:
-        c.wait()
+    for i in range(n):
+        for p in range(refs[i].shape[0]):
+            pltpu.make_async_copy(refs[i].at[p], refs[n + i].at[p], sem.at[i]).start()
+    for i in range(n):
+        pltpu.make_async_copy(refs[i], refs[n + i], sem.at[i]).wait()
 
 
 def kernel(n_gx, n_gy, n_gz, owner_in, state, phi_in, nst, dsol, res,
@@ -131,28 +131,35 @@
         c.start()
         return c
 
-    loads = {}
-    for i in (0, 1, 14, 15, 2, 3, 4, 5, 6, 7, 8, 9, 10, 11, 12, 13):
-        c = pltpu.make_async_copy(state.at[:, i], q1.at[:, rows_of(i)], lsem.at[i])
-        c.start()
-        loads[i] = c
-    phi_load = pltpu.make_async_copy(phi_in, phi, lsem.at[CX])
+    for i in range(CX):
+        pltpu.make_async_copy(state.at[:, i], q1.at[:, rows_of(i)], lsem.at[0]).start()
+    phi_load = pltpu.make_async_copy(phi_in, phi, lsem.at[1])
     phi_load.start()
-    owner_load = pltpu.make_async_copy(owner_in, owner_ref, lsem.at[CX + 1])
+    owner_load = pltpu.make_async_copy(owner_in, owner_ref, lsem.at[2])
     owner_load.start()
 
+    def wait_for(ref, sem):
+        pltpu.make_async_copy(ref, ref, sem).wait()
+
+    n_zy = n_gz // 2
+
+    def flat(h):
+        return {"gz": (gz // n_zy) * n_zy + lax.rem(gz + h, n_zy)}
+
     barrier = pltpu.get_barrier_semaphore()
-    peers = [x_lo, x_hi, y_lo, y_hi, z_lo, z_hi, at("gy", gy, n_gy, n_gy // 2), at("gz", gz, n_gz, n_gz // 2)]
+    peers = [x_lo, x_hi, y_lo, y_hi, z_lo, z_hi, at("gy", gy, n_gy, n_gy // 2), at("gz", gz, n_gz, n_zy)]
     for dev in peers:
         pl.semaphore_signal(barrier, inc=1, device_id=dev, device_id_type=MESH)
 
-    pending = []
-
-    def send_x(q, r):
+    def send_x_first():
+        return [remote(state.at[:, pl.ds(CX - 2, 2)], xh.at[0, 0], hs.at[0, 0], hr.at[0, 0], x_hi),
+                remote(state.at[:, pl.ds(0, 2)], xh.at[0, 1], hs.at[0, 0], hr.at[0, 0], x_lo)]
+
+    def send_x_second():
         cs = []
         for j in (0, 1):
-            cs.append(remote(q.at[:, rows_of(14 + j)], xh.at[r, 0, j], hs.at[r, j], hr.at[r, j], x_hi))
-            cs.append(remote(q.at[:, rows_of(j)], xh.at[r, 1, j], hs.at[r, 2 + j], hr.at[r, 2 + j], x_lo))
+            cs.append(remote(q2.at[:, rows_of(14 + j)], xh.at[1, 0, :, j], hs.at[1, 0], hr.at[1, 0], x_hi))
+            cs.append(remote(q2.at[:, rows_of(j)], xh.at[1, 1, :, j], hs.at[1, 0], hr.at[1, 0], x_lo))
         return cs
 
     def pack_y(q, r):
@@ -168,20 +175,25 @@
 
     def pack_outer(q, r):
         acc = pack_z(lambda k, i: q[k, rows_of(i), :], tuple(zpack[r, k] for k in range(NF)), (0, 1, 14, 15), 1)
-        low = (lanes((8, CZ)) & 7) < 4
         for k in range(NF):
             zpack[r, k] = acc[k]
-            top, bottom = acc[k][0:8], acc[k][8:16]
-            zsend[r, 1, k] = jnp.where(low, top, pltpu.roll(bottom, 4, 1))
-            zsend[r, 0, k] = jnp.where(low, pltpu.roll(top, CZ - 4, 1), bottom)
+        slot = (lanes((8, CZ)) & 7) >> 1
+        for g in range(NF // 2 + 1):
+            parts = [acc[k][8 * h:8 * h + 8] for k in (2 * g, 2 * g + 1) if k < NF for h in (0, 1)]
+            for side, lane in ((1, 2), (0, 4)):
+                v = pltpu.roll(parts[0], CZ - lane, 1)
+                for n in range(1, len(parts)):
+                    shift = (CZ + 2 * n - lane) % CZ
+                    v = jnp.where(slot == n, pltpu.roll(parts[n], shift, 1) if shift else parts[n], v)
+                zsend[r, side, g] = v
 
     def send_y(r):
-        return [remote(ysend.at[r, 1], yrecv.at[r, 0], hs.at[r, 4], hr.at[r, 4], y_hi),
-                remote(ysend.at[r, 0], yrecv.at[r, 1], hs.at[r, 5], hr.at[r, 5], y_lo)]
+        return [remote(ysend.at[r, 1], yrecv.at[r, 0], hs.at[r, 1], hr.at[r, 1], y_hi),
+                remote(ysend.at[r, 0], yrecv.at[r, 1], hs.at[r, 1], hr.at[r, 1], y_lo)]
 
     def send_z(r):
-        return [remote(zsend.at[r, 1], zrecv.at[r, 0], hs.at[r, 6], hr.at[r, 6], z_hi),
-                remote(zsend.at[r, 0], zrecv.at[r, 1], hs.at[r, 7], hr.at[r, 7], z_lo)]
+        return [remote(zsend.at[r, 1], zrecv.at[r, 0], hs.at[r, 2], hr.at[r, 2], z_hi),
+                remote(zsend.at[r, 0], zrecv.at[r, 1], hs.at[r, 2], hr.at[r, 2], z_lo)]
 
     def interior(q):
         def speed_body(i):
@@ -251,13 +263,16 @@
             f = interface_flux(lambda k: z_shifted(cells[k]), s, pltpu.roll(s, CZ - 1, 1), 3)
             return [pltpu.roll(f[k], 1, 1) - f[k] for k in range(NF)]
 
+        def received(side, lane, k):
+            m = zrecv[r, side, k // 2]
+            shifts = [(2 * CZ + lane - 2 * (2 * (k % 2) + h)) % CZ for h in (0, 1)]
+            return jnp.concatenate([pltpu.roll(m, t, 1) if t else m for t in shifts], axis=0)
+
         def from_left(k):
-            m = zrecv[r, 0, k]
-            return jnp.concatenate([m, pltpu.roll(m, CZ - 4, 1)], axis=0)
+            return received(0, 2, k)
 
         def from_right(k):
-            m = zrecv[r, 1, k]
-            return jnp.concatenate([pltpu.roll(m, 4, 1), m], axis=0)
+            return received(1, 4, k)
 
         left = z_edge([jnp.where(low, from_left(k), zpack[r, k]) for k in range(NF)])
         for k in range(NF):
@@ -275,9 +290,9 @@
     def x_part(q, r, finish):
         def get(i):
             if i < 0:
-                return lambda k: xh[r, 0, i + 2, k]
+                return lambda k: xh[r, 0, k, i + 2]
             if i >= CX:
-                return lambda k: xh[r, 1, i - CX, k]
+                return lambda k: xh[r, 1, k, i - CX]
             return lambda k: q[k, rows_of(i), :]
 
         def speed(i):
@@ -309,16 +324,14 @@
         for k in range(NF):
             nst[k, i] = 0.5 * q1[k, rows_of(i), :] + 0.5 * (q2[k, rows_of(i), :] + DTH * t[k])
 
-    for i in range(CX):
-        loads[i].wait()
+    pl.semaphore_wait(barrier, len(peers))
+    send_x_first()
+    wait_for(q1.at[:, pl.ds(0, CX * CY)], lsem.at[0])
     pack_inner(q1, 0)
     pack_outer(q1, 0)
-    pl.semaphore_wait(barrier, len(peers))
-    zs = send_z(0)
-    xs = send_x(q1, 0)
+    send_z(0)
     pack_y(q1, 0)
-    ys = send_y(0)
-    pending += xs + ys + zs
+    send_y(0)
 
     phi_load.wait()
     owner_load.wait()
@@ -339,87 +352,74 @@
                 pb[o, b, j] = v
         each(HALF, phi_body)
     interior(q1)
-    for c in ys:
-        c.wait_recv()
+    wait_for(yrecv.at[0], hr.at[0, 1])
     y_part(q1, 0)
-    p1 = [remote(pb.at[2, 0], pfirst.at[0], ps.at[0], pr.at[0], x_hi),
-          remote(pb.at[2, 1], pfirst.at[1], ps.at[1], pr.at[1], x_lo)]
-    for c in zs:
-        c.wait_recv()
+    remote(pb.at[2, 0], pfirst.at[0], ps.at[0], pr.at[0], x_hi)
+    remote(pb.at[2, 1], pfirst.at[1], ps.at[0], pr.at[0], x_lo)
+    wait_for(zrecv.at[0], hr.at[0, 2])
     z_part(0)
     rest(finish_first)
     pack_inner(q2, 1)
-    for c in xs:
-        c.wait_recv()
+    wait_for(xh.at[0], hr.at[0, 0])
     x_part(q1, 0, finish_first)
 
     pack_outer(q2, 1)
-    zs = send_z(1)
-    xs = send_x(q2, 1)
+    send_z(1)
+    send_x_second()
     pack_y(q2, 1)
-    ys = send_y(1)
-    pending += xs + ys + zs
+    send_y(1)
 
     interior(q2)
-    for c in ys:
-        c.wait_recv()
+    wait_for(yrecv.at[1], hr.at[1, 1])
     y_part(q2, 1)
-    p2 = [remote(pb.at[1, 1], pin.at[0, 1], ps.at[2], pr.at[2], x_hi),
-          remote(pb.at[3, 0], pin.at[1, 0], ps.at[3], pr.at[3], x_lo)]
-    for c in p1:
-        c.wait_recv()
+    remote(pb.at[1, 1], pin.at[0, 1], ps.at[1], pr.at[1], x_hi)
+    remote(pb.at[3, 0], pin.at[1, 0], ps.at[1], pr.at[1], x_lo)
+    wait_for(zrecv.at[1], hr.at[1, 2])
+    z_part(1)
+    rest(finish_new)
+    wait_for(pfirst, pr.at[0])
 
     def add_body(j):
         pb[1, 0, j] = pb[1, 0, j] + pfirst[0, j]
         pb[3, 1, j] = pb[3, 1, j] + pfirst[1, j]
 
     each(HALF, add_body)
-    p2 += [remote(pb.at[1, 0], pin.at[0, 0], ps.at[4], pr.at[4], x_hi),
-           remote(pb.at[3, 1], pin.at[1, 1], ps.at[5], pr.at[5], x_lo)]
-    pending += p1 + p2
-    for c in zs:
-        c.wait_recv()
-    z_part(1)
-    rest(finish_new)
-    for c in xs:
-        c.wait_recv()
+    wait_for(xh.at[1], hr.at[1, 0])
     x_part(q2, 1, finish_new)
-
-    d1 = [remote(nst.at[0, pl.ds(0, HALF)], gl.at[0], ds_.at[0], dr.at[0], x_hi),
-          remote(nst.at[0, pl.ds(HALF, HALF)], gr.at[1], ds_.at[1], dr.at[1], x_lo),
-          remote(nst.at[0, pl.ds(HALF, HALF)], gl.at[1], ds_.at[2], dr.at[2], x_hi),
-          remote(nst.at[0, pl.ds(0, HALF)], gr.at[0], ds_.at[3], dr.at[3], x_lo)]
 
     def mass_body(i, acc):
         return acc + nst[0, i, 0:8, :] + nst[0, i, 8:16, :]
 
-    m0[...] = lax.fori_loop(0, CX, mass_body, jnp.zeros((8, CZ), jnp.float32), unroll=4)
-
-    def spread(src, dst, devices, first):
-        return [remote(src, dst.at[t], ms.at[first + t], mr.at[first + t], dev) for t, dev in enumerate(devices)]
-
-    def gathered(copies, own, got, n):
-        for c in copies:
-            c.wait_recv()
+    acc = lax.fori_loop(0, CX, mass_body, jnp.zeros((8, CZ), jnp.float32), unroll=4)
+    m0[...] = jnp.sum(acc, axis=0, keepdims=True)
+
+    def spread(src, dst, devices, t):
+        for n, dev in enumerate(devices):
+            remote(src, dst.at[n], ms.at[t], mr.at[t], dev)
+
+    def gathered(own, got, t):
+        wait_for(got, mr.at[t])
         acc = own[...]
-        for o in range(n - 1):
-            acc = acc + got[o]
+        for n in range(got.shape[0]):
+            acc = acc + got[n]
         return acc
 
-    n_zy = n_gz // 2
-    along_y = [{"gz": (gz // n_zy) * n_zy + lax.rem(gz + o, n_zy)} for o in range(1, n_zy)]
     along_z = [{**at("gx", gx, n_gx, o), **at("gz", gz, n_gz, h * n_zy)}
                for o in range(n_gx) for h in (0, 1) if o + h > 0]
-    m_x = spread(m0, mx, [at("gy", gy, n_gy, o) for o in range(1, n_gy)], 0)
-
-    m1[...] = gathered(m_x, m0, mx, n_gy)
-    m_y = spread(m1, my, along_y, n_gy - 1)
-    m2[...] = gathered(m_y, m1, my, n_zy)
-    m_z = spread(m2, mz, along_z, n_gy + n_zy - 2)
-    pending += m_y + m_z + m_x
-
-    for c in p2:
-        c.wait_recv()
+    spread(m0, mz, along_z, 0)
+
+    remote(pb.at[1, 0], pin.at[0, 0], ps.at[1], pr.at[1], x_hi)
+    remote(pb.at[3, 1], pin.at[1, 1], ps.at[1], pr.at[1], x_lo)
+
+    remote(nst.at[0, pl.ds(0, HALF)], gl.at[0], ds_.at[0], dr.at[0], x_hi)
+    remote(nst.at[0, pl.ds(HALF, HALF)], gr.at[1], ds_.at[0], dr.at[1], x_lo)
+    remote(nst.at[0, pl.ds(HALF, HALF)], gl.at[1], ds_.at[0], dr.at[2], x_hi)
+    remote(nst.at[0, pl.ds(0, HALF)], gr.at[0], ds_.at[0], dr.at[4], x_lo)
+
+    m1[...] = gathered(m0, mz, 0)
+    spread(m1, mx, [at("gy", gy, n_gy, o) for o in range(1, n_gy)], 1)
+
+    wait_for(pin, pr.at[1])
 
     def pot_body(j):
         for b in (0, 1):
@@ -432,50 +432,23 @@
 
     each(CX, row_body)
     pzs[0] = pack_z(lambda k, i: pot[i], blank(1), range(0, CX), 4)[0]
-    ph = [remote(pot.at[CX - 1], pxr.at[0], fs.at[0], fr.at[0], x_hi),
-          remote(pot.at[0], pxr.at[1], fs.at[1], fr.at[1], x_lo),
-          remote(pys.at[1], pyr.at[0], fs.at[2], fr.at[2], y_hi),
-          remote(pys.at[0], pyr.at[1], fs.at[3], fr.at[3], y_lo),
-          remote(pzs.at[0], pzr.at[0], fs.at[4], fr.at[4], z_hi),
-          remote(pzs.at[0], pzr.at[1], fs.at[5], fr.at[5], z_lo)]
-    pending += ph
-
-    d1[0].wait_recv()
-    d2 = [remote(gl.at[0], go.at[0], ds_.at[4], dr.at[4], x_hi)]
-    d1[1].wait_recv()
-    d2 += [remote(gr.at[1], go.at[1], ds_.at[5], dr.at[5], x_lo)]
-
-    for c in ph:
-        c.wait_recv()
-    lane = lanes()
-    row = lax.broadcasted_iota(jnp.int32, (CY, CZ), 0)
-    halo = jnp.where((lane & 7) < 4, pzr[0, :, :], pzr[1, :, :])
-
-    def lap(i, below, above):
-        p = pot[i]
-        h = pltpu.roll(halo, lax.rem(CZ - 4 - 8 * i + CZ, CZ), 1)
-        z = pltpu.roll(jnp.where(lane == CZ - 1, h, p), 1, 1) + pltpu.roll(jnp.where(lane == 0, h, p), CZ - 1, 1)
-        up = jnp.where(row == 0, pyr[0, pl.ds(i, 1), :], pltpu.roll(p, 1, 0))
-        dn = jnp.where(row == CY - 1, pyr[1, pl.ds(i, 1), :], pltpu.roll(p, CY - 1, 0))
-        res[i] = FOURPIG * nst[0, i] - (((below + above) + (up + dn) + z) - 6.0 * p)
-
-    lap(0, pxr[0], pot[1])
-
-    def lap_body(j):
-        lap(j + 1, pot[j], pot[j + 2])
-    each(CX - 2, lap_body, 7)
-    lap(CX - 1, pot[CX - 2], pxr[1])
-
-    total = gathered(m_z, m2, mz, len(along_z) + 1)
-    cells = float(CX * CY * CZ * n_gx * n_gy * n_gz)
-    mean = jnp.sum(total) * (FOURPIG / cells)
-
-    def mean_body(i):
-        res[i] = res[i] - mean
-    each(CX, mean_body)
-
-    for c in (d1[2], d1[3]):
-        c.wait_recv()
+    remote(pot.at[CX - 1], pxr.at[0], fs.at[0], fr.at[0], x_hi)
+    remote(pot.at[0], pxr.at[1], fs.at[0], fr.at[0], x_lo)
+    remote(pys.at[1], pyr.at[0], fs.at[1], fr.at[1], y_hi)
+    remote(pys.at[0], pyr.at[1], fs.at[1], fr.at[1], y_lo)
+    remote(pzs.at[0], pzr.at[0], fs.at[2], fr.at[2], z_hi)
+    remote(pzs.at[0], pzr.at[1], fs.at[2], fr.at[2], z_lo)
+
+    wait_for(gl.at[0], dr.at[0])
+    remote(gl.at[0], go.at[0], ds_.at[1], dr.at[3], x_hi)
+    wait_for(gr.at[1], dr.at[1])
+    remote(gr.at[1], go.at[1], ds_.at[1], dr.at[3], x_lo)
+
+    m2[...] = gathered(m1, mx, 1)
+    spread(m2, my, [flat(h) for h in range(1, n_zy)], 2)
+
+    wait_for(gl.at[1], dr.at[2])
+    wait_for(gr.at[0], dr.at[4])
 
     def is_box(o, b, s):
         return is_code(lax.rem(gx + o, n_gx) * 2 + b, s)
@@ -490,9 +463,33 @@
                 v = v + boxes[t] * near[s][t]
             dsol[s, j] = v
     each(HALF, near_body)
+    total = gathered(m2, my, 2)
+    cells = float(CX * CY * CZ * n_gx * n_gy * n_gz)
+    mean = jnp.sum(total) / cells
+
+    for n, ref in enumerate((pxr, pyr, pzr)):
+        wait_for(ref, fr.at[n])
+    lane = lanes()
+    row = lax.broadcasted_iota(jnp.int32, (CY, CZ), 0)
+    halo = jnp.where((lane & 7) < 4, pzr[0, :, :], pzr[1, :, :])
+
+    def lap(i, below, above):
+        p = pot[i]
+        h = pltpu.roll(halo, lax.rem(CZ - 4 - 8 * i + CZ, CZ), 1)
+        z = pltpu.roll(jnp.where(lane == CZ - 1, h, p), 1, 1) + pltpu.roll(jnp.where(lane == 0, h, p), CZ - 1, 1)
+        up = jnp.where(row == 0, pyr[0, pl.ds(i, 1), :], pltpu.roll(p, 1, 0))
+        dn = jnp.where(row == CY - 1, pyr[1, pl.ds(i, 1), :], pltpu.roll(p, CY - 1, 0))
+        res[i] = FOURPIG * (nst[0, i] - mean) - (((below + above) + (up + dn) + z) - 6.0 * p)
+
+    lap(0, pxr[0], pot[1])
+
+    def lap_body(j):
+        lap(j + 1, pot[j], pot[j + 2])
+    each(CX - 2, lap_body, 7)
+    lap(CX - 1, pot[CX - 2], pxr[1])
+
     far = [[is_box(2, b, s) for b in (0, 1)] for s in range(SLOTS)]
-    for c in d2:
-        c.wait_recv()
+    wait_for(go, dr.at[3])
 
     def far_body(j):
         boxes = [go[0, j], go[1, j]]
@@ -500,9 +497,12 @@
             dsol[s, j] = dsol[s, j] + (boxes[0] * far[s][0] + boxes[1] * far[s][1])
     each(HALF, far_body)
 
-    pending += d1 + d2
-    for c in pending:
-        c.wait_send()
+    for r in (0, 1):
+        for n, ref in enumerate((xh, yrecv, zrecv)):
+            wait_for(ref.at[r], hs.at[r, n])
+    for ref, sem in ((pfirst, ps.at[0]), (pin, ps.at[1]), (pin, ds_.at[0]), (go, ds_.at[1]), (mz, ms.at[0]), (mx, ms.at[1]), (my, ms.at[2]),
+                     (pxr, fs.at[0]), (pyr, fs.at[1]), (pzr, fs.at[2])):
+        wait_for(ref, sem)
 
 
 def solution(mesh):
@@ -512,7 +512,6 @@
         f32 = jnp.float32
         V = lambda *s: pltpu.VMEM(s, f32)
         D = lambda *s: pltpu.SemaphoreType.DMA(s)
-        n_mass = 2 * n_gx + n_gy + n_gz // 2 - 3
         hbm = pl.BlockSpec(memory_space=pltpu.HBM)
         vmem = pl.BlockSpec(memory_space=pltpu.VMEM)
         outs = pl.pallas_call(
@@ -529,14 +528,14 @@
                 V(NF, ROWS, CZ), V(NF, ROWS, CZ), V(SLOTS, HALF, CY, CZ),
                 V(CX, CY, CZ), V(ROWS, CZ), V(CX, CY, CZ), V(NF, CX, CY, CZ),
                 V(2, NF, CY, CZ), V(NF, CX, CZ), V(NF, CY, CZ),
-                V(2, 2, 2, NF, CY, CZ), V(2, 2, NF, 2, CX, CZ), V(2, 2, NF, 2, CX, CZ),
-                V(2, NF, CY, CZ), V(2, 2, NF, 8, CZ), V(2, 2, NF, 8, CZ),
+                V(2, 2, NF, 2, CY, CZ), V(2, 2, NF, 2, CX, CZ), V(2, 2, NF, 2, CX, CZ),
+                V(2, NF, CY, CZ), V(2, 2, NF // 2 + 1, 8, CZ), V(2, 2, NF // 2 + 1, 8, CZ),
                 V(4, 2, HALF, CY, CZ), V(CX, CY, CZ), V(2, 2, HALF, CY, CZ), V(2, HALF, CY, CZ),
                 V(2, HALF, CY, CZ), V(2, HALF, CY, CZ), V(2, HALF, CY, CZ),
                 V(2, CY, CZ), V(2, CX, CZ), V(2, CX, CZ), V(1, CY, CZ), V(2, CY, CZ),
-                V(8, CZ), V(8, CZ), V(8, CZ),
-                V(n_gy - 1, 8, CZ), V(n_gz // 2 - 1, 8, CZ), V(2 * n_gx - 1, 8, CZ),
-                D(CX + 2), D(2, 8), D(2, 8), D(6), D(6), D(6), D(6), D(6), D(6), D(n_mass), D(n_mass),
+                V(1, CZ), V(1, CZ), V(1, CZ),
+                V(n_gy - 1, 1, CZ), V(n_gz // 2 - 1, 1, CZ), V(2 * n_gx - 1, 1, CZ),
+                D(3), D(2, 3), D(2, 3), D(2), D(2), D(2), D(5), D(3), D(3), D(3), D(3),
             ],
             compiler_params=pltpu.CompilerParams(
                 collective_id=0, has_side_effects=True, vmem_limit_bytes=32 * 1024 * 1024

time: 44.6 us -> 42.6 us (0.955)
  Pallas kernels: 43.8 us -> 41.9 us
    pallas_call x1, Pallas kernels: 42.7 us -> 40.8 us  [on_device(): pl.pallas_call(functools.partial(kernel, n_gx, n_gy, n_gz), out_shape=(ja...]
where the time goes in v2:
time: 42.6 us; the launch traced here: 42.5 us
  Pallas kernels  41.9 us (98%)
  between operations  0.64 us (2%)
    pallas_call x1, Pallas kernels, on_device(): pl.pallas_call(functools.partial(kernel, n_gx, n_gy, n_gz), out_shape=(ja...  40.8 us
    pallas_call x1, Pallas kernels, on_device(): pl.pallas_call(move_out, out_shape=tuple((jax.ShapeDtypeStruct(o.shape, f...  1.07 us

profile of v2, /device:TPU:1, one launch (start us, length us, event | category | flops | bytes accessed | tf_op | source)
XLA Modules:
  0.0 42.5 jit_solution(7877310072956162644)
XLA Ops:
  0.6 40.8 %gas_step.1 = (f32[7,16,16,128]{3,2,1,0:T(8,128)S(1)}, f32[4,8,16,128]{3,2,1,0:T(8,128)S(1)}, f32[16,16,128]{2,1,0:T(8,128)S(1)}) custom-call(s32[1,1,8]{2,1,0:T(1,128)} %owner_in.1, f32[7,16,16,128]{3,2,1,0:T(8,128)} %state.1, f32[4,8,16,128]{3,2,1,0:T(8,128)} %phi_in.1), custom_call_target="tpu_custom_call" | custom-call | tf_op jit(solution)/shard_map/gas_step/pallas_call | solution.py:517
  41.4 1.1 %move_out.1 = (f32[7,16,16,128]{3,2,1,0:T(8,128)}, f32[4,8,16,128]{3,2,1,0:T(8,128)}, f32[16,16,128]{2,1,0:T(8,128)}) custom-call(f32[7,16,16,128]{3,2,1,0:T(8,128)S(1)} %get-tuple-element.6.refs_0_, f32[4,8,16,128]{3,2,1,0:T(8,128)S(1)} %get-tuple-element.7.refs_1_, f32[16,16,128]{2,1,0:T(8,128)S(1)} %get-tuple-element.8.refs_2_), custom_call_target="tpu_custom_call" | custom-call | tf_op jit(solution)/shard_map/move_out/pallas_call | solution.py:549

commit v3 on v2

--- a/solution.py
+++ b/solution.py
@@ -131,6 +131,16 @@
         c.start()
         return c
 
+    n_zy = n_gz // 2
+
+    def flat(h):
+        return {"gz": (gz // n_zy) * n_zy + lax.rem(gz + h, n_zy)}
+
+    barrier = pltpu.get_barrier_semaphore()
+    peers = [x_lo, x_hi, y_lo, y_hi, z_lo, z_hi, at("gy", gy, n_gy, n_gy // 2), at("gz", gz, n_gz, n_zy)]
+    for dev in peers:
+        pl.semaphore_signal(barrier, inc=1, device_id=dev, device_id_type=MESH)
+
     for i in range(CX):
         pltpu.make_async_copy(state.at[:, i], q1.at[:, rows_of(i)], lsem.at[0]).start()
     phi_load = pltpu.make_async_copy(phi_in, phi, lsem.at[1])
@@ -140,16 +150,6 @@
 
     def wait_for(ref, sem):
         pltpu.make_async_copy(ref, ref, sem).wait()
-
-    n_zy = n_gz // 2
-
-    def flat(h):
-        return {"gz": (gz // n_zy) * n_zy + lax.rem(gz + h, n_zy)}
-
-    barrier = pltpu.get_barrier_semaphore()
-    peers = [x_lo, x_hi, y_lo, y_hi, z_lo, z_hi, at("gy", gy, n_gy, n_gy // 2), at("gz", gz, n_gz, n_zy)]
-    for dev in peers:
-        pl.semaphore_signal(barrier, inc=1, device_id=dev, device_id_type=MESH)
 
     def send_x_first():
         return [remote(state.at[:, pl.ds(CX - 2, 2)], xh.at[0, 0], hs.at[0, 0], hr.at[0, 0], x_hi),
@@ -231,7 +231,7 @@
         for k in range(NF):
             fb[1, k] = f[k]
 
-    def y_part(q, r):
+    def y_part(q, r, finish):
         for k in range(NF):
             for j in (0, 1):
                 q[k, pl.ds(BASE - 2 + j, CX, stride=PITCH), :] = yrecv[r, 0, k, j]
@@ -245,15 +245,27 @@
             fym[k] = f[k]
         first_row = lax.broadcasted_iota(jnp.int32, (CY, CZ), 0) == 0
 
-        def y_body(i):
+        def y_tendency(i):
             at_ = i * PITCH + BASE
             f = interface_flux(lambda k: tuple(q[k, pl.ds(at_ + o, CY), :] for o in (-1, 0, 1, 2)),
                                sy[pl.ds(at_, CY), :], sy[pl.ds(at_ + 1, CY), :], 2)
             for k in range(NF):
                 lower = jnp.where(first_row, fym[k, pl.ds(i, 1), :], pltpu.roll(f[k], 1, 0))
-                dd[k, i] = dd[k, i] + (lower - f[k])
-
-        each(CX, y_body, UN)
+                f[k] = dd[k, i] + (lower - f[k])
+            return f
+
+        def outer_body(j):
+            i = jnp.where(j < 2, j, j + 12)
+            t = y_tendency(i)
+            for k in range(NF):
+                dd[k, i] = t[k]
+
+        each(4, outer_body, UN)
+
+        def inner_body(j):
+            finish(j + 2, y_tendency(j + 2))
+
+        each(CX - 4, inner_body, UN)
 
     def z_part(r):
         low = (lanes() & 7) < 4
@@ -281,11 +293,14 @@
         for k in range(NF):
             tz[k] = jnp.where(low, right[k], tz[k])
 
-    def tendency(i, k):
+    def edge_tendency(i, k):
         lane = lanes()
         outer = (lane < 2) | (lane >= CZ - 2)
         shift = (2 * CZ - 4 - 8 * i) % CZ if isinstance(i, int) else lax.rem(2 * CZ - 4 - 8 * i, CZ)
-        return dd[k, i] + jnp.where(outer, pltpu.roll(tz[k], shift, 1), 0.0)
+        return jnp.where(outer, pltpu.roll(tz[k], shift, 1), 0.0)
+
+    def tendency(i, k):
+        return dd[k, i] + edge_tendency(i, k)
 
     def x_part(q, r, finish):
         def get(i):
@@ -311,10 +326,18 @@
         b = flux(15)
         finish(15, [tendency(15, k) + (a[k] - b[k]) for k in range(NF)])
 
-    def rest(finish):
+    def edges(scale, view, fields):
         def body(j):
-            finish(2 + j, [tendency(2 + j, k) for k in range(NF)])
+            for k in fields:
+                ref, idx = view(j + 2, k)
+                ref[idx] = ref[idx] + scale * edge_tendency(j + 2, k)
         each(CX - 4, body, UN)
+
+    def edges_packed(r, scale):
+        lane = lanes()
+        here = (lane >= 16) & (lane < CZ - 16) & ((lane & 7) >= 2) & ((lane & 7) < 6)
+        for k in range(NF):
+            zpack[r, k] = zpack[r, k] + jnp.where(here, scale * tz[k], 0.0)
 
     def finish_first(i, t):
         for k in range(NF):
@@ -353,30 +376,28 @@
         each(HALF, phi_body)
     interior(q1)
     wait_for(yrecv.at[0], hr.at[0, 1])
-    y_part(q1, 0)
+    y_part(q1, 0, finish_first)
     remote(pb.at[2, 0], pfirst.at[0], ps.at[0], pr.at[0], x_hi)
     remote(pb.at[2, 1], pfirst.at[1], ps.at[0], pr.at[0], x_lo)
+    pack_inner(q2, 1)
     wait_for(zrecv.at[0], hr.at[0, 2])
     z_part(0)
-    rest(finish_first)
-    pack_inner(q2, 1)
+    edges_packed(1, DTH)
     wait_for(xh.at[0], hr.at[0, 0])
     x_part(q1, 0, finish_first)
 
     pack_outer(q2, 1)
     send_z(1)
     send_x_second()
+    edges(DTH, lambda i, k: (q2, (k, rows_of(i), slice(None))), range(NF))
     pack_y(q2, 1)
     send_y(1)
 
     interior(q2)
     wait_for(yrecv.at[1], hr.at[1, 1])
-    y_part(q2, 1)
+    y_part(q2, 1, finish_new)
     remote(pb.at[1, 1], pin.at[0, 1], ps.at[1], pr.at[1], x_hi)
     remote(pb.at[3, 0], pin.at[1, 0], ps.at[1], pr.at[1], x_lo)
-    wait_for(zrecv.at[1], hr.at[1, 2])
-    z_part(1)
-    rest(finish_new)
     wait_for(pfirst, pr.at[0])
 
     def add_body(j):
@@ -384,6 +405,9 @@
         pb[3, 1, j] = pb[3, 1, j] + pfirst[1, j]
 
     each(HALF, add_body)
+    wait_for(zrecv.at[1], hr.at[1, 2])
+    z_part(1)
+    edges(0.5 * DTH, lambda i, k: (nst, (k, i)), (0,))
     wait_for(xh.at[1], hr.at[1, 0])
     x_part(q2, 1, finish_new)
 
@@ -407,7 +431,6 @@
     along_z = [{**at("gx", gx, n_gx, o), **at("gz", gz, n_gz, h * n_zy)}
                for o in range(n_gx) for h in (0, 1) if o + h > 0]
     spread(m0, mz, along_z, 0)
-
     remote(pb.at[1, 0], pin.at[0, 0], ps.at[1], pr.at[1], x_hi)
     remote(pb.at[3, 1], pin.at[1, 1], ps.at[1], pr.at[1], x_lo)
 
@@ -415,6 +438,7 @@
     remote(nst.at[0, pl.ds(HALF, HALF)], gr.at[1], ds_.at[0], dr.at[1], x_lo)
     remote(nst.at[0, pl.ds(HALF, HALF)], gl.at[1], ds_.at[0], dr.at[2], x_hi)
     remote(nst.at[0, pl.ds(0, HALF)], gr.at[0], ds_.at[0], dr.at[4], x_lo)
+    edges(0.5 * DTH, lambda i, k: (nst, (k, i)), range(1, NF))
 
     m1[...] = gathered(m0, mz, 0)
     spread(m1, mx, [at("gy", gy, n_gy, o) for o in range(1, n_gy)], 1)

time: 42.6 us -> 42.8 us (level)
  no operation moved by 1% of the time
where the time goes in v3:
time: 42.8 us; the launch traced here: 42.7 us
  Pallas kernels  42.1 us (98%)
  between operations  0.64 us (1%)
    pallas_call x1, Pallas kernels, on_device(): pl.pallas_call(functools.partial(kernel, n_gx, n_gy, n_gz), out_shape=(ja...  41 us
    pallas_call x1, Pallas kernels, on_device(): pl.pallas_call(move_out, out_shape=tuple((jax.ShapeDtypeStruct(o.shape, f...  1.07 us

profile of v3, /device:TPU:1, one launch (start us, length us, event | category | flops | bytes accessed | tf_op | source)
XLA Modules:
  0.0 42.7 jit_solution(15029852216344283503)
XLA Ops:
  0.6 41.0 %gas_step.1 = (f32[7,16,16,128]{3,2,1,0:T(8,128)S(1)}, f32[4,8,16,128]{3,2,1,0:T(8,128)S(1)}, f32[16,16,128]{2,1,0:T(8,128)S(1)}) custom-call(s32[1,1,8]{2,1,0:T(1,128)} %owner_in.1, f32[7,16,16,128]{3,2,1,0:T(8,128)} %state.1, f32[4,8,16,128]{3,2,1,0:T(8,128)} %phi_in.1), custom_call_target="tpu_custom_call" | custom-call | tf_op jit(solution)/shard_map/gas_step/pallas_call | solution.py:541
  41.6 1.1 %move_out.1 = (f32[7,16,16,128]{3,2,1,0:T(8,128)}, f32[4,8,16,128]{3,2,1,0:T(8,128)}, f32[16,16,128]{2,1,0:T(8,128)}) custom-call(f32[7,16,16,128]{3,2,1,0:T(8,128)S(1)} %get-tuple-element.6.refs_0_, f32[4,8,16,128]{3,2,1,0:T(8,128)S(1)} %get-tuple-element.7.refs_1_, f32[16,16,128]{2,1,0:T(8,128)S(1)} %get-tuple-element.8.refs_2_), custom_call_target="tpu_custom_call" | custom-call | tf_op jit(solution)/shard_map/move_out/pallas_call | solution.py:573

commit v4 on v3

--- a/solution.py
+++ b/solution.py
@@ -85,14 +85,14 @@
     lane = lanes()
 
     def put(i, acc, shift):
-        here = (lane >= 8 * i) & (lane < 8 * i + 8)
+        here = (lane >= CZ - 8 - 8 * i) & (lane < CZ - 8 * i)
         return tuple(jnp.where(here, pltpu.roll(load(k, i), shift, 1), a) for k, a in enumerate(acc))
 
     if isinstance(slabs, tuple):
         for i in slabs:
-            acc = put(i, acc, (8 * i + 4) % CZ)
+            acc = put(i, acc, CZ - 4 - 8 * i)
         return acc
-    return lax.fori_loop(slabs.start, slabs.stop, lambda i, a: put(i, a, lax.rem(8 * i + 4, CZ)), acc, unroll=unroll)
+    return lax.fori_loop(slabs.start, slabs.stop, lambda i, a: put(i, a, CZ - 4 - 8 * i), acc, unroll=unroll)
 
 
 def blank(count):
@@ -296,11 +296,20 @@
     def edge_tendency(i, k):
         lane = lanes()
         outer = (lane < 2) | (lane >= CZ - 2)
-        shift = (2 * CZ - 4 - 8 * i) % CZ if isinstance(i, int) else lax.rem(2 * CZ - 4 - 8 * i, CZ)
-        return jnp.where(outer, pltpu.roll(tz[k], shift, 1), 0.0)
+        return jnp.where(outer, pltpu.roll(tz[k], 4 + 8 * i, 1), 0.0)
 
     def tendency(i, k):
         return dd[k, i] + edge_tendency(i, k)
+
+    def edges_rows(scale):
+        lane = lanes((CX, CZ))
+        x = lax.broadcasted_iota(jnp.int32, (CX, CZ), 0)
+        here = ((lane < 2) | (lane >= CZ - 2)) & (x >= 2) & (x < CX - 2)
+        for k in range(NF):
+            for side, j in ((0, 0), (0, 1), (1, 0), (1, 1)):
+                row = jnp.broadcast_to(tz[k, 14 * side + j:14 * side + j + 1, :], (CX, CZ))
+                part = pltpu.roll(row, 4, 1, stride=8, stride_axis=0)
+                ysend[1, side, k, j] = ysend[1, side, k, j] + jnp.where(here, scale * part, 0.0)
 
     def x_part(q, r, finish):
         def get(i):
@@ -331,7 +340,7 @@
             for k in fields:
                 ref, idx = view(j + 2, k)
                 ref[idx] = ref[idx] + scale * edge_tendency(j + 2, k)
-        each(CX - 4, body, UN)
+        each(CX - 4, body, 6)
 
     def edges_packed(r, scale):
         lane = lanes()
@@ -389,9 +398,10 @@
     pack_outer(q2, 1)
     send_z(1)
     send_x_second()
+    pack_y(q2, 1)
+    edges_rows(DTH)
+    send_y(1)
     edges(DTH, lambda i, k: (q2, (k, rows_of(i), slice(None))), range(NF))
-    pack_y(q2, 1)
-    send_y(1)
 
     interior(q2)
     wait_for(yrecv.at[1], hr.at[1, 1])
@@ -455,7 +465,7 @@
         pys[1, pl.ds(i, 1), :] = pot[i, CY - 1:CY, :]
 
     each(CX, row_body)
-    pzs[0] = pack_z(lambda k, i: pot[i], blank(1), range(0, CX), 4)[0]
+    pzs[0] = pack_z(lambda k, i: pot[i], blank(1), range(0, CX), 16)[0]
     remote(pot.at[CX - 1], pxr.at[0], fs.at[0], fr.at[0], x_hi)
     remote(pot.at[0], pxr.at[1], fs.at[0], fr.at[0], x_lo)
     remote(pys.at[1], pyr.at[0], fs.at[1], fr.at[1], y_hi)
@@ -499,7 +509,7 @@
 
     def lap(i, below, above):
         p = pot[i]
-        h = pltpu.roll(halo, lax.rem(CZ - 4 - 8 * i + CZ, CZ), 1)
+        h = pltpu.roll(halo, 4 + 8 * i, 1)
         z = pltpu.roll(jnp.where(lane == CZ - 1, h, p), 1, 1) + pltpu.roll(jnp.where(lane == 0, h, p), CZ - 1, 1)
         up = jnp.where(row == 0, pyr[0, pl.ds(i, 1), :], pltpu.roll(p, 1, 0))
         dn = jnp.where(row == CY - 1, pyr[1, pl.ds(i, 1), :], pltpu.roll(p, CY - 1, 0))

time: 42.8 us -> 42.2 us (0.986)
  Pallas kernels: 42.1 us -> 41.4 us
    pallas_call x1, Pallas kernels: 41 us -> 40.4 us  [on_device(): pl.pallas_call(functools.partial(kernel, n_gx, n_gy, n_gz), out_shape=(ja...]
where the time goes in v4:
time: 42.2 us; the launch traced here: 42.1 us
  Pallas kernels  41.4 us (98%)
  between operations  0.64 us (2%)
    pallas_call x1, Pallas kernels, on_device(): pl.pallas_call(functools.partial(kernel, n_gx, n_gy, n_gz), out_shape=(ja...  40.4 us
    pallas_call x1, Pallas kernels, on_device(): pl.pallas_call(move_out, out_shape=tuple((jax.ShapeDtypeStruct(o.shape, f...  1.07 us

profile of v4, /device:TPU:1, one launch (start us, length us, event | category | flops | bytes accessed | tf_op | source)
XLA Modules:
  0.0 42.1 jit_solution(11932111525769770531)
XLA Ops:
  0.6 40.4 %gas_step.1 = (f32[7,16,16,128]{3,2,1,0:T(8,128)S(1)}, f32[4,8,16,128]{3,2,1,0:T(8,128)S(1)}, f32[16,16,128]{2,1,0:T(8,128)S(1)}) custom-call(s32[1,1,8]{2,1,0:T(1,128)} %owner_in.1, f32[7,16,16,128]{3,2,1,0:T(8,128)} %state.1, f32[4,8,16,128]{3,2,1,0:T(8,128)} %phi_in.1), custom_call_target="tpu_custom_call" | custom-call | tf_op jit(solution)/shard_map/gas_step/pallas_call | solution.py:551
  41.0 1.1 %move_out.1 = (f32[7,16,16,128]{3,2,1,0:T(8,128)}, f32[4,8,16,128]{3,2,1,0:T(8,128)}, f32[16,16,128]{2,1,0:T(8,128)}) custom-call(f32[7,16,16,128]{3,2,1,0:T(8,128)S(1)} %get-tuple-element.6.refs_0_, f32[4,8,16,128]{3,2,1,0:T(8,128)S(1)} %get-tuple-element.7.refs_1_, f32[16,16,128]{2,1,0:T(8,128)S(1)} %get-tuple-element.8.refs_2_), custom_call_target="tpu_custom_call" | custom-call | tf_op jit(solution)/shard_map/move_out/pallas_call | solution.py:583

commit v5 on v4

--- a/solution.py
+++ b/solution.py
@@ -17,7 +17,7 @@
 ROWS = CX * PITCH + 8
 HALF = 8
 SLOTS = 4
-UN = 2
+UN = 4
 
 
 def pressure(q5):
@@ -497,10 +497,6 @@
                 v = v + boxes[t] * near[s][t]
             dsol[s, j] = v
     each(HALF, near_body)
-    total = gathered(m2, my, 2)
-    cells = float(CX * CY * CZ * n_gx * n_gy * n_gz)
-    mean = jnp.sum(total) / cells
-
     for n, ref in enumerate((pxr, pyr, pzr)):
         wait_for(ref, fr.at[n])
     lane = lanes()
@@ -513,7 +509,7 @@
         z = pltpu.roll(jnp.where(lane == CZ - 1, h, p), 1, 1) + pltpu.roll(jnp.where(lane == 0, h, p), CZ - 1, 1)
         up = jnp.where(row == 0, pyr[0, pl.ds(i, 1), :], pltpu.roll(p, 1, 0))
         dn = jnp.where(row == CY - 1, pyr[1, pl.ds(i, 1), :], pltpu.roll(p, CY - 1, 0))
-        res[i] = FOURPIG * (nst[0, i] - mean) - (((below + above) + (up + dn) + z) - 6.0 * p)
+        res[i] = FOURPIG * nst[0, i] - (((below + above) + (up + dn) + z) - 6.0 * p)
 
     lap(0, pxr[0], pot[1])
 
@@ -521,6 +517,14 @@
         lap(j + 1, pot[j], pot[j + 2])
     each(CX - 2, lap_body, 7)
     lap(CX - 1, pot[CX - 2], pxr[1])
+
+    total = gathered(m2, my, 2)
+    cells = float(CX * CY * CZ * n_gx * n_gy * n_gz)
+    mean = jnp.sum(total) / cells
+
+    def mean_body(i):
+        res[i] = res[i] - FOURPIG * mean
+    each(CX, mean_body, 8)
 
     far = [[is_box(2, b, s) for b in (0, 1)] for s in range(SLOTS)]
     wait_for(go, dr.at[3])

time: 42.2 us -> 41.7 us (0.988)
    pallas_call x1, Pallas kernels: 40.4 us -> 39.9 us  [on_device(): pl.pallas_call(functools.partial(kernel, n_gx, n_gy, n_gz), out_shape=(ja...]
where the time goes in v5:
time: 41.7 us; the launch traced here: 41.6 us
  Pallas kernels  41 us (98%)
  between operations  0.64 us (2%)
    pallas_call x1, Pallas kernels, on_device(): pl.pallas_call(functools.partial(kernel, n_gx, n_gy, n_gz), out_shape=(ja...  39.9 us
    pallas_call x1, Pallas kernels, on_device(): pl.pallas_call(move_out, out_shape=tuple((jax.ShapeDtypeStruct(o.shape, f...  1.07 us

profile of v5, /device:TPU:1, one launch (start us, length us, event | category | flops | bytes accessed | tf_op | source)
XLA Modules:
  0.0 41.6 jit_solution(9396456774277890876)
XLA Ops:
  0.6 39.9 %gas_step.1 = (f32[7,16,16,128]{3,2,1,0:T(8,128)S(1)}, f32[4,8,16,128]{3,2,1,0:T(8,128)S(1)}, f32[16,16,128]{2,1,0:T(8,128)S(1)}) custom-call(s32[1,1,8]{2,1,0:T(1,128)} %owner_in.1, f32[7,16,16,128]{3,2,1,0:T(8,128)} %state.1, f32[4,8,16,128]{3,2,1,0:T(8,128)} %phi_in.1), custom_call_target="tpu_custom_call" | custom-call | tf_op jit(solution)/shard_map/gas_step/pallas_call | solution.py:555
  40.5 1.1 %move_out.1 = (f32[7,16,16,128]{3,2,1,0:T(8,128)}, f32[4,8,16,128]{3,2,1,0:T(8,128)}, f32[16,16,128]{2,1,0:T(8,128)}) custom-call(f32[7,16,16,128]{3,2,1,0:T(8,128)S(1)} %get-tuple-element.6.refs_0_, f32[4,8,16,128]{3,2,1,0:T(8,128)S(1)} %get-tuple-element.7.refs_1_, f32[16,16,128]{2,1,0:T(8,128)S(1)} %get-tuple-element.8.refs_2_), custom_call_target="tpu_custom_call" | custom-call | tf_op jit(solution)/shard_map/move_out/pallas_call | solution.py:587

commit v6 on v5

--- a/solution.py
+++ b/solution.py
@@ -14,7 +14,7 @@
 NF = 7
 CX, CY, CZ = 16, 16, 128
 PITCH, BASE = 24, 8
-ROWS = CX * PITCH + 8
+ROWS = CX * PITCH + 32
 HALF = 8
 SLOTS = 4
 UN = 4
@@ -414,7 +414,7 @@
         pb[1, 0, j] = pb[1, 0, j] + pfirst[0, j]
         pb[3, 1, j] = pb[3, 1, j] + pfirst[1, j]
 
-    each(HALF, add_body)
+    each(HALF, add_body, 4)
     wait_for(zrecv.at[1], hr.at[1, 2])
     z_part(1)
     edges(0.5 * DTH, lambda i, k: (nst, (k, i)), (0,))
@@ -459,12 +459,12 @@
         for b in (0, 1):
             pot[b * HALF + j] = pb[0, b, j] + (pin[0, b, j] + pin[1, b, j])
 
-    each(HALF, pot_body)
+    each(HALF, pot_body, 4)
     def row_body(i):
         pys[0, pl.ds(i, 1), :] = pot[i, 0:1, :]
         pys[1, pl.ds(i, 1), :] = pot[i, CY - 1:CY, :]
 
-    each(CX, row_body)
+    each(CX, row_body, 8)
     pzs[0] = pack_z(lambda k, i: pot[i], blank(1), range(0, CX), 16)[0]
     remote(pot.at[CX - 1], pxr.at[0], fs.at[0], fr.at[0], x_hi)
     remote(pot.at[0], pxr.at[1], fs.at[0], fr.at[0], x_lo)
@@ -496,7 +496,7 @@
             for t in range(1, 6):
                 v = v + boxes[t] * near[s][t]
             dsol[s, j] = v
-    each(HALF, near_body)
+    each(HALF, near_body, 2)
     for n, ref in enumerate((pxr, pyr, pzr)):
         wait_for(ref, fr.at[n])
     lane = lanes()
@@ -533,7 +533,7 @@
         boxes = [go[0, j], go[1, j]]
         for s in range(SLOTS):
             dsol[s, j] = dsol[s, j] + (boxes[0] * far[s][0] + boxes[1] * far[s][1])
-    each(HALF, far_body)
+    each(HALF, far_body, 4)
 
     for r in (0, 1):
         for n, ref in enumerate((xh, yrecv, zrecv)):

time: 41.7 us -> 41.6 us (level)
  no operation moved by 1% of the time
where the time goes in v6:
time: 41.6 us; the launch traced here: 41.5 us
  Pallas kernels  40.9 us (98%)
  between operations  0.64 us (2%)
    pallas_call x1, Pallas kernels, on_device(): pl.pallas_call(functools.partial(kernel, n_gx, n_gy, n_gz), out_shape=(ja...  39.8 us
    pallas_call x1, Pallas kernels, on_device(): pl.pallas_call(move_out, out_shape=tuple((jax.ShapeDtypeStruct(o.shape, f...  1.07 us

profile of v6, /device:TPU:1, one launch (start us, length us, event | category | flops | bytes accessed | tf_op | source)
XLA Modules:
  0.0 41.5 jit_solution(17060213016117201091)
XLA Ops:
  0.6 39.8 %gas_step.1 = (f32[7,16,16,128]{3,2,1,0:T(8,128)S(1)}, f32[4,8,16,128]{3,2,1,0:T(8,128)S(1)}, f32[16,16,128]{2,1,0:T(8,128)S(1)}) custom-call(s32[1,1,8]{2,1,0:T(1,128)} %owner_in.1, f32[7,16,16,128]{3,2,1,0:T(8,128)} %state.1, f32[4,8,16,128]{3,2,1,0:T(8,128)} %phi_in.1), custom_call_target="tpu_custom_call" | custom-call | tf_op jit(solution)/shard_map/gas_step/pallas_call | solution.py:555
  40.5 1.1 %move_out.1 = (f32[7,16,16,128]{3,2,1,0:T(8,128)}, f32[4,8,16,128]{3,2,1,0:T(8,128)}, f32[16,16,128]{2,1,0:T(8,128)}) custom-call(f32[7,16,16,128]{3,2,1,0:T(8,128)S(1)} %get-tuple-element.6.refs_0_, f32[4,8,16,128]{3,2,1,0:T(8,128)S(1)} %get-tuple-element.7.refs_1_, f32[16,16,128]{2,1,0:T(8,128)S(1)} %get-tuple-element.8.refs_2_), custom_call_target="tpu_custom_call" | custom-call | tf_op jit(solution)/shard_map/move_out/pallas_call | solution.py:587

commit v7 on v5

--- a/solution.py
+++ b/solution.py
@@ -359,11 +359,11 @@
     pl.semaphore_wait(barrier, len(peers))
     send_x_first()
     wait_for(q1.at[:, pl.ds(0, CX * CY)], lsem.at[0])
+    pack_y(q1, 0)
+    send_y(0)
     pack_inner(q1, 0)
     pack_outer(q1, 0)
     send_z(0)
-    pack_y(q1, 0)
-    send_y(0)
 
     phi_load.wait()
     owner_load.wait()

time: 41.7 us -> 42.4 us (1.017)
  Pallas kernels: 41 us -> 41.7 us
    pallas_call x1, Pallas kernels: 39.9 us -> 40.6 us  [on_device(): pl.pallas_call(functools.partial(kernel, n_gx, n_gy, n_gz), out_shape=(ja...]
where the time goes in v7:
time: 42.4 us; the launch traced here: 42.3 us
  Pallas kernels  41.7 us (98%)
  between operations  0.64 us (2%)
    pallas_call x1, Pallas kernels, on_device(): pl.pallas_call(functools.partial(kernel, n_gx, n_gy, n_gz), out_shape=(ja...  40.6 us
    pallas_call x1, Pallas kernels, on_device(): pl.pallas_call(move_out, out_shape=tuple((jax.ShapeDtypeStruct(o.shape, f...  1.07 us

profile of v7, /device:TPU:1, one launch (start us, length us, event | category | flops | bytes accessed | tf_op | source)
XLA Modules:
  0.0 42.3 jit_solution(7069240321023853528)
XLA Ops:
  0.6 40.6 %gas_step.1 = (f32[7,16,16,128]{3,2,1,0:T(8,128)S(1)}, f32[4,8,16,128]{3,2,1,0:T(8,128)S(1)}, f32[16,16,128]{2,1,0:T(8,128)S(1)}) custom-call(s32[1,1,8]{2,1,0:T(1,128)} %owner_in.1, f32[7,16,16,128]{3,2,1,0:T(8,128)} %state.1, f32[4,8,16,128]{3,2,1,0:T(8,128)} %phi_in.1), custom_call_target="tpu_custom_call" | custom-call | tf_op jit(solution)/shard_map/gas_step/pallas_call | solution.py:555
  41.3 1.1 %move_out.1 = (f32[7,16,16,128]{3,2,1,0:T(8,128)}, f32[4,8,16,128]{3,2,1,0:T(8,128)}, f32[16,16,128]{2,1,0:T(8,128)}) custom-call(f32[7,16,16,128]{3,2,1,0:T(8,128)S(1)} %get-tuple-element.6.refs_0_, f32[4,8,16,128]{3,2,1,0:T(8,128)S(1)} %get-tuple-element.7.refs_1_, f32[16,16,128]{2,1,0:T(8,128)S(1)} %get-tuple-element.8.refs_2_), custom_call_target="tpu_custom_call" | custom-call | tf_op jit(solution)/shard_map/move_out/pallas_call | solution.py:587

commit v8 on v6

--- a/solution.py
+++ b/solution.py
@@ -415,6 +415,8 @@
         pb[3, 1, j] = pb[3, 1, j] + pfirst[1, j]
 
     each(HALF, add_body, 4)
+    remote(pb.at[1, 0, pl.ds(0, 4)], pin.at[0, 0, pl.ds(0, 4)], ps.at[1], pr.at[1], x_hi)
+    remote(pb.at[3, 1, pl.ds(0, 4)], pin.at[1, 1, pl.ds(0, 4)], ps.at[1], pr.at[1], x_lo)
     wait_for(zrecv.at[1], hr.at[1, 2])
     z_part(1)
     edges(0.5 * DTH, lambda i, k: (nst, (k, i)), (0,))
@@ -441,8 +443,8 @@
     along_z = [{**at("gx", gx, n_gx, o), **at("gz", gz, n_gz, h * n_zy)}
                for o in range(n_gx) for h in (0, 1) if o + h > 0]
     spread(m0, mz, along_z, 0)
-    remote(pb.at[1, 0], pin.at[0, 0], ps.at[1], pr.at[1], x_hi)
-    remote(pb.at[3, 1], pin.at[1, 1], ps.at[1], pr.at[1], x_lo)
+    remote(pb.at[1, 0, pl.ds(4, 4)], pin.at[0, 0, pl.ds(4, 4)], ps.at[1], pr.at[1], x_hi)
+    remote(pb.at[3, 1, pl.ds(4, 4)], pin.at[1, 1, pl.ds(4, 4)], ps.at[1], pr.at[1], x_lo)
 
     remote(nst.at[0, pl.ds(0, HALF)], gl.at[0], ds_.at[0], dr.at[0], x_hi)
     remote(nst.at[0, pl.ds(HALF, HALF)], gr.at[1], ds_.at[0], dr.at[1], x_lo)

time: 41.6 us -> 41.6 us (level)
  no operation moved by 1% of the time
where the time goes in v8:
time: 41.6 us; the launch traced here: 41.5 us
  Pallas kernels  40.8 us (98%)
  between operations  0.64 us (2%)
    pallas_call x1, Pallas kernels, on_device(): pl.pallas_call(functools.partial(kernel, n_gx, n_gy, n_gz), out_shape=(ja...  39.8 us
    pallas_call x1, Pallas kernels, on_device(): pl.pallas_call(move_out, out_shape=tuple((jax.ShapeDtypeStruct(o.shape, f...  1.07 us

profile of v8, /device:TPU:1, one launch (start us, length us, event | category | flops | bytes accessed | tf_op | source)
XLA Modules:
  0.0 41.5 jit_solution(7397082266370559619)
XLA Ops:
  0.6 39.8 %gas_step.1 = (f32[7,16,16,128]{3,2,1,0:T(8,128)S(1)}, f32[4,8,16,128]{3,2,1,0:T(8,128)S(1)}, f32[16,16,128]{2,1,0:T(8,128)S(1)}) custom-call(s32[1,1,8]{2,1,0:T(1,128)} %owner_in.1, f32[7,16,16,128]{3,2,1,0:T(8,128)} %state.1, f32[4,8,16,128]{3,2,1,0:T(8,128)} %phi_in.1), custom_call_target="tpu_custom_call" | custom-call | tf_op jit(solution)/shard_map/gas_step/pallas_call | solution.py:557
  40.4 1.1 %move_out.1 = (f32[7,16,16,128]{3,2,1,0:T(8,128)}, f32[4,8,16,128]{3,2,1,0:T(8,128)}, f32[16,16,128]{2,1,0:T(8,128)}) custom-call(f32[7,16,16,128]{3,2,1,0:T(8,128)S(1)} %get-tuple-element.6.refs_0_, f32[4,8,16,128]{3,2,1,0:T(8,128)S(1)} %get-tuple-element.7.refs_1_, f32[16,16,128]{2,1,0:T(8,128)S(1)} %get-tuple-element.8.refs_2_), custom_call_target="tpu_custom_call" | custom-call | tf_op jit(solution)/shard_map/move_out/pallas_call | solution.py:589
